TPU v7x, 32 devices: a whole 2x2x4 slice. The times are simulated.
32 devices in a mesh: tm: 32 (over z, y, x, core).
Axes of the slice: x: 2, y: 2, z: 4, core: 2. Of those that a mesh axis runs over, the one named last changes fastest.
Arguments:
- field: bfloat16 [10752, 2048], P('tm'), may hold values from -52 to 52
- index: float32 [10752, 10], P('tm'), may hold values from -13 to 13
- lag_list: int32 [61], replicated, may hold values from -30 to 30, as said below
- index_offset: int32 [10], replicated, may hold values from 0 to 14, as said below
- sea_mask: int32 [2048], P('tm'), may hold values 0 or 1
Outputs:
- corr_maps: float32 [2048, 10, 61], P('tm')
Inputs may be any that keep to these rules, and one draw needn't show every extreme that they name: `lag_list`: each whole number of -30 to 30 appears once. `index_offset`: some index has the extra lead 14.
All inputs are finite; a program needn't handle non-finite values. No bound on the sum of `sea_mask` on one device may be relied on, other than what follows from the above.
Results may differ from a plain program's by a relative error of at most 0.00051.
Values may be sent and summed in bfloat16 or wider, within the bound.
A program may use at most 256 MiB of HBM per device.

v0:
```python
import functools

import jax
import jax.numpy as jnp
from jax import lax
from jax.experimental import pallas as pl
from jax.experimental.pallas import tpu as pltpu
from jax.sharding import PartitionSpec as P

MAXLAG = 30
MAXOFF = 14
PLACES = 2 * MAXLAG + MAXOFF + 1
MESH = pl.DeviceIdType.MESH


def round_up(value, unit):
    return -(-value // unit) * unit


def kernel(
    sizes,
    field_hbm,
    index_ref,
    lag_ref,
    offset_ref,
    mask_ref,
    out_ref,
    field_ref,
    idx_ref,
    recv,
    idx_all,
    win,
    acc,
    acc_in,
    field_send,
    field_recv,
    one_send,
    one_recv,
    two_send,
    two_recv,
    last_send,
    last_recv,
    own_sem,
):
    devices, t_dev, kcount, kpad, rows, low = sizes
    chips = devices // 2
    high = chips // low
    lanes = idx_ref.shape[1]
    wide = lanes + 128
    me = lax.axis_index("tm")
    chip = lax.div(me, 2)
    core = lax.rem(me, 2)
    hi = lax.div(chip, low)
    lo = lax.rem(chip, low)
    partner = chip * 2 + (1 - core)
    cells = recv.shape[2]

    def across(step):
        other, bit = 0, 1
        while bit < chips:
            flip = lax.rem(lax.div(chip, bit) + lax.div(step, bit), 2)
            other, bit = other + flip * bit, bit * 2
        return other

    def slot_of(device):
        at = lax.div(device, 2)
        return (lax.rem(device, 2) * low + lax.rem(at, low)) * high + lax.div(at, low)

    def block(at):
        return field_ref.at[:, pl.ds(pl.multiple_of(at * cells, cells), cells)]

    my_slot = slot_of(me)

    def one_copy(step):
        to = lax.rem(hi + step, high)
        return pltpu.make_async_remote_copy(
            src_ref=idx_ref,
            dst_ref=idx_all.at[my_slot],
            send_sem=one_send.at[step],
            recv_sem=one_recv.at[step],
            device_id=((to * low + lo) * 2 + core,),
            device_id_type=MESH,
        )

    def two_copy(step):
        to = lax.rem(lo + step, low)
        part = idx_all.at[pl.ds((core * low + lo) * high, high)]
        return pltpu.make_async_remote_copy(
            src_ref=part,
            dst_ref=part,
            send_sem=two_send.at[step],
            recv_sem=two_recv.at[step],
            device_id=((hi * low + to) * 2 + core,),
            device_id_type=MESH,
        )

    def last_copy():
        part = idx_all.at[pl.ds(core * chips, chips)]
        return pltpu.make_async_remote_copy(
            src_ref=part,
            dst_ref=part,
            send_sem=last_send.at[0],
            recv_sem=last_recv.at[0],
            device_id=(partner,),
            device_id_type=MESH,
        )

    def field_copy(step):
        to = across(step)
        return pltpu.make_async_remote_copy(
            src_ref=block(to),
            dst_ref=recv.at[step],
            send_sem=field_send.at[step],
            recv_sem=field_recv.at[step],
            device_id=(to * 2 + core,),
            device_id_type=MESH,
        )

    def each(low_step, high_step, act):
        def body(step, carry):
            act(step)
            return carry

        lax.fori_loop(low_step, high_step, body, 0)

    load = pltpu.make_async_copy(field_hbm, field_ref, own_sem.at[2])
    load.start()
    barrier = pltpu.get_barrier_semaphore()

    def greet(device):
        pl.semaphore_signal(barrier, inc=1, device_id=(device,), device_id_type=MESH)

    each(1, chips, lambda s: greet(across(s) * 2 + core))
    greet(partner)
    idx_ref[...] = jnp.zeros_like(idx_ref)
    idx_ref[0:kcount, 0:t_dev] = index_ref[...]
    acc[...] = jnp.zeros_like(acc)
    pl.semaphore_wait(barrier, chips)
    load.wait()
    own_idx = pltpu.make_async_copy(idx_ref, idx_all.at[my_slot], own_sem.at[0])
    own_field = pltpu.make_async_copy(block(chip), recv.at[0], own_sem.at[1])
    own_idx.start()
    own_field.start()
    each(1, high, lambda s: one_copy(s).start())
    each(1, chips, lambda s: field_copy(s).start())
    own_idx.wait()
    own_field.wait()
    each(1, high, lambda s: one_copy(s).wait())
    each(1, low, lambda s: two_copy(s).start())
    each(1, low, lambda s: two_copy(s).wait())
    last_copy().start()
    last_copy().wait()

    total_days = devices * t_dev * 1.0

    def sum_body(at, carry):
        first, second = carry
        value = idx_all[at]
        return first + value, second + value * value

    zero = jnp.zeros((kpad, lanes), jnp.float32)
    first, second = lax.fori_loop(0, devices, sum_body, (zero, zero))
    mean = jnp.sum(first, 1, keepdims=True) / total_days
    var = jnp.sum(second, 1, keepdims=True) / total_days - mean * mean
    valid = lax.broadcasted_iota(jnp.int32, (kpad, lanes), 1) < t_dev

    def center_body(at, carry):
        value = (idx_all[at] - mean).astype(jnp.bfloat16).astype(jnp.float32)
        value = jnp.where(valid, value, 0.0)
        idx_all[at] = value
        return carry + value

    centered_sum = jnp.sum(lax.fori_loop(0, devices, center_body, zero), 1, keepdims=True)
    day = lax.broadcasted_iota(jnp.int32, (lanes, 128), 0)
    shift = lax.broadcasted_iota(jnp.int32, (lanes, 128), 1) - MAXLAG
    late = jnp.where((day >= t_dev - shift) & (day < t_dev), 1.0, 0.0).astype(jnp.bfloat16)
    early = jnp.where(day < -shift, 1.0, 0.0).astype(jnp.bfloat16)
    dropped = jnp.dot(
        idx_all[slot_of(devices - 1)].astype(jnp.bfloat16),
        late,
        preferred_element_type=jnp.float32,
    ) + jnp.dot(
        idx_all[0].astype(jnp.bfloat16), early, preferred_element_type=jnp.float32
    )
    fill = jnp.zeros((round_up(kpad, 8) - kpad, 128), jnp.float32)
    totals = jnp.transpose(jnp.concatenate([centered_sum - dropped, fill], 0))

    place = lax.broadcasted_iota(jnp.int32, (kpad, wide), 1)
    tail = jnp.zeros((kpad, 128), jnp.float32)
    reach = 64

    def window_body(step, carry):
        device = across(step) * 2 + core
        before = idx_all[slot_of(jnp.maximum(device - 1, 0))]
        after = idx_all[slot_of(jnp.minimum(device + 1, devices - 1))]
        before = before * jnp.where(device > 0, 1.0, 0.0)
        after = after * jnp.where(device < devices - 1, 1.0, 0.0)
        here = jnp.concatenate([idx_all[slot_of(device)], tail], 1)
        before = jnp.concatenate([before, tail], 1)
        after = jnp.concatenate([after, tail], 1)
        left = pltpu.roll(before, (reach - t_dev) % wide, 1)
        mid = pltpu.roll(here, reach, 1)
        right = pltpu.roll(after, reach + t_dev, 1)
        ext = jnp.where(place < reach, left, jnp.where(place < reach + t_dev, mid, right))
        for k in range(kcount):
            line = jnp.broadcast_to(ext[k : k + 1], (rows, wide))
            turned = pltpu.roll(line, wide - reach - MAXLAG, 1, stride=1, stride_axis=0)
            win[step, k * rows : (k + 1) * rows, :] = turned[:, :lanes].astype(jnp.bfloat16)
        return carry

    def source_body(step, carry):
        @pl.when(step > 0)
        def _():
            field_copy(step).wait()

        got = recv[step]
        add_products(step, 0, count)
        add_sums(got)
        return carry

    count = kcount * rows

    def add_products(step, begin, end):
        acc[begin:end, :] += jnp.dot(
            win[step, begin:end, :t_dev], recv[step], preferred_element_type=jnp.float32
        )

    def add_sums(got):
        value = got.astype(jnp.float32)
        acc[kcount * rows : kcount * rows + 1, :] += jnp.sum(value, 0, keepdims=True)
        acc[kcount * rows + 1 : kcount * rows + 2, :] += jnp.sum(value * value, 0, keepdims=True)

    lax.fori_loop(0, chips, window_body, 0)
    lax.fori_loop(0, chips - 1, source_body, 0)

    def swap(place, begin, end):
        return pltpu.make_async_remote_copy(
            src_ref=acc.at[pl.ds(begin, end - begin)],
            dst_ref=acc_in.at[pl.ds(begin, end - begin)],
            send_sem=last_send.at[place],
            recv_sem=last_recv.at[place],
            device_id=(partner,),
            device_id_type=MESH,
        )

    middle = kcount // 2 * rows
    field_copy(chips - 1).wait()
    add_sums(recv[chips - 1])
    swaps = [swap(1, count, count + 8), swap(2, 0, middle), swap(3, middle, count)]
    swaps[0].start()
    add_products(chips - 1, 0, middle)
    swaps[1].start()
    add_products(chips - 1, middle, count)
    swaps[2].start()
    swaps[0].wait()
    half = cells // 2

    def mine(begin, end):
        total = acc[begin:end, :] + acc_in[begin:end, :]
        return jnp.where(core == 0, total[:, :half], total[:, half:])

    mean_x = mine(count, count + 1) / total_days
    var_x = mine(count + 1, count + 2) / total_days - mean_x * mean_x
    inner = total_days * jnp.sqrt(var_x + 1e-06)
    mask = mask_ref[...].astype(jnp.float32)
    outer = jnp.sqrt(var + 1e-06)
    lag = lag_ref[...]
    row = lax.broadcasted_iota(jnp.int32, (rows, lag.shape[1]), 0)
    for k in range(kcount):
        if k == 0:
            swaps[1].wait()
        if k == kcount // 2:
            swaps[2].wait()
        numer = mine(k * rows, (k + 1) * rows) - mean_x * totals[0:rows, k : k + 1]
        value = numer / (inner * outer[k : k + 1]) * mask
        chosen = jnp.where(row == lag + (offset_ref[k] + MAXLAG), 1.0, 0.0)
        out_ref[k] = lax.dot_general(
            value,
            chosen,
            (((0,), (0,)), ((), ())),
            precision=lax.Precision.HIGHEST,
            preferred_element_type=jnp.float32,
        )


def shards(field, index, lag_list, index_offset, sea_mask):
    t_dev, cells_all = field.shape
    devices = lax.axis_size("tm")
    kcount = index.shape[1]
    kpad = kcount
    lanes = round_up(t_dev, 128)
    rows = round_up(PLACES, 16)
    chips = devices // 2
    cells = cells_all // chips
    low = 1
    while low * low < chips:
        low *= 2
    high = chips // low
    sizes = (devices, t_dev, kcount, kpad, rows, low)
    dma = pltpu.SemaphoreType.DMA
    f32 = jnp.float32
    held = 4 * cells_all * t_dev + 4 * devices * round_up(kcount, 8) * lanes
    held += 2 * chips * kcount * rows * lanes + 8 * (kcount * rows + 8) * cells
    limit = held + 4 * 1024 * 1024
    vmem = pl.BlockSpec(memory_space=pltpu.VMEM)
    maps = pl.pallas_call(
        functools.partial(kernel, sizes),
        out_shape=jax.ShapeDtypeStruct((kcount, cells // 2, lag_list.shape[0]), f32),
        in_specs=[
            pl.BlockSpec(memory_space=pl.ANY),
            vmem,
            vmem,
            pl.BlockSpec(memory_space=pltpu.SMEM),
            vmem,
        ],
        out_specs=vmem,
        scratch_shapes=[
            pltpu.VMEM((t_dev, cells_all), jnp.bfloat16),
            pltpu.VMEM((kpad, lanes), f32),
            pltpu.VMEM((chips, t_dev, cells), jnp.bfloat16),
            pltpu.VMEM((devices, kpad, lanes), f32),
            pltpu.VMEM((chips, kcount * rows, lanes), jnp.bfloat16),
            pltpu.VMEM((kcount * rows + 8, cells), f32),
            pltpu.VMEM((kcount * rows + 8, cells), f32),
            dma((chips,)),
            dma((chips,)),
            dma((high,)),
            dma((high,)),
            dma((low,)),
            dma((low,)),
            dma((4,)),
            dma((4,)),
            dma((3,)),
        ],
        compiler_params=pltpu.CompilerParams(
            collective_id=0, has_side_effects=True, vmem_limit_bytes=60 * 1024 * 1024
        ),
    )(field, index.T, lag_list[None, :], index_offset, sea_mask[None, :])
    return jnp.transpose(maps, (1, 0, 2))


def solution(mesh):
    return jax.shard_map(
        shards,
        mesh=mesh,
        in_specs=(P("tm", None), P("tm", None), P(), P(), P("tm")),
        out_specs=P("tm", None, None),
        check_vma=False,
    )
```

profile of v0, /device:TPU:9, one launch (start us, length us, event | category | flops | bytes accessed | tf_op | source)
XLA Modules:
  0.0 44.0 jit_solution(1845498674088280262)
XLA Ops:
  0.0 42.3 %shard_map.55 = f32[10,64,61]{2,1,0:T(8,128)} custom-call(bf16[336,2048]{1,0:T(8,128)(2,1)} %field_hbm.1, f32[10,336]{1,0:T(8,128)} %bitcast.5, s32[1,61]{1,0:T(1,128)} %bitcast.6, s32[10]{0:T(128)} %offset_ref.1, s32[1,64]{1,0:T(1,128)} %bitcast.7), custom_call_target="tpu_custom_call" | custom-call | tf_op jit(solution)/shard_map/pallas_call | solution.py:306
  42.3 1.7 %copy.7 = f32[64,10,61]{2,0,1:T(8,128)} copy(f32[64,10,61]{2,0,1:T(8,128)} %bitcast.4) | data formatting | bytes 312320
where the time goes:
time: 44.2 us; the launch traced here: 44 us
  Pallas kernels  42.3 us (96%)
  local copies, waits for them, and re-layouts  1.72 us (4%)
    pallas_call x1, Pallas kernels, shards(): pl.pallas_call(functools.partial(kernel, sizes), out_shape=jax.ShapeDtype...  42.3 us
    unnamed x1, local copies, waits for them, and re-layouts  1.72 us

commit v1 on v0

v1 whole, which is shorter than its diff:
```python
import functools

import jax
import jax.numpy as jnp
from jax import lax
from jax.experimental import pallas as pl
from jax.experimental.pallas import tpu as pltpu
from jax.sharding import PartitionSpec as P

MAXLAG = 30
MAXOFF = 14
REACH = 64
ROWS = 64
EXTRA = 8
TOP = 32767.0
GROUPS = 4
MESH = pl.DeviceIdType.MESH


def round_up(value, unit):
    return -(-value // unit) * unit


def kernel(
    sizes,
    field_hbm,
    index_ref,
    lag_ref,
    offset_ref,
    mask_ref,
    out_ref,
    field_ref,
    idx_ref,
    idx_all,
    zmsg,
    zin,
    recv,
    win,
    acc,
    other,
    partner_in,
    sent,
    sent_extra,
    got,
    got_extra,
    small,
    tot_ref,
    raw_send,
    raw_recv,
    idx_send,
    idx_recv,
    relay_sem,
    z_send,
    z_recv,
    swap_send,
    swap_recv,
    sum_send,
    sum_recv,
    own_sem,
    round_sem,
):
    devices, t_dev, kcount, groups, g = sizes
    lanes = idx_ref.shape[1]
    wide = lanes + 128
    half_k = kcount // 2
    count = half_k * ROWS
    cells = 128
    me = lax.axis_index("tm")
    core = lax.rem(me, 2)
    chip = lax.div(me, 2)
    h = lax.div(chip, g)
    m = lax.rem(chip, g)
    partner = chip * 2 + (1 - core)
    f32 = jnp.float32
    total_days = devices * t_dev * 1.0

    def across(step):
        other_m, bit = 0, 1
        while bit < g:
            flip = lax.rem(lax.div(m, bit) + lax.div(step, bit), 2)
            other_m, bit = other_m + flip * bit, bit * 2
        return other_m

    def device_of(group, member):
        return (group * g + member) * 2 + core

    def remote(src, dst, send, recv_s, device):
        return pltpu.make_async_remote_copy(
            src_ref=src,
            dst_ref=dst,
            send_sem=send,
            recv_sem=recv_s,
            device_id=(device,),
            device_id_type=MESH,
        )

    def block(at):
        return field_ref.at[:, pl.ds(pl.multiple_of(at * cells, cells), cells)]

    def plane_of(piece):
        return lax.rem(h + 1 + piece, groups)

    def raw_copy(piece, step):
        to = across(step)
        return remote(
            block(plane_of(piece) * g + to),
            recv.at[piece, step],
            raw_send.at[piece, step],
            raw_recv.at[piece, step],
            device_of(h, to),
        )

    def own_copy(piece):
        return pltpu.make_async_copy(
            block(plane_of(piece) * g + m), recv.at[piece, 0], own_sem.at[piece]
        )

    def idx_copy(step):
        return remote(
            idx_ref,
            idx_all.at[core * g + m],
            idx_send.at[step],
            idx_recv.at[step],
            device_of(h, across(step)),
        )

    def relay_copy():
        part = idx_all.at[pl.ds(core * g, g)]
        return remote(part, part, relay_sem.at[0], relay_sem.at[1], partner)

    def z_copy(step):
        return remote(
            zmsg,
            zin.at[step],
            z_send.at[step],
            z_recv.at[step],
            device_of(lax.rem(h + step, groups), m),
        )

    def swap_copy(piece):
        return remote(
            other.at[piece],
            partner_in.at[piece],
            swap_send.at[piece],
            swap_recv.at[piece],
            partner,
        )

    def sum_copy(piece):
        return remote(
            sent.at[piece],
            got.at[piece],
            sum_send.at[0, piece],
            sum_recv.at[0, piece],
            device_of(plane_of(piece), m),
        )

    def extra_copy(piece):
        return remote(
            sent_extra.at[piece],
            got_extra.at[piece],
            sum_send.at[1, piece],
            sum_recv.at[1, piece],
            device_of(plane_of(piece), m),
        )

    def each(low_step, high_step, act):
        def body(step, carry):
            act(step)
            return carry

        lax.fori_loop(low_step, high_step, body, 0)

    load = pltpu.make_async_copy(field_hbm, field_ref, own_sem.at[groups])
    load.start()
    barrier = pltpu.get_barrier_semaphore()

    def tell(sem, device):
        pl.semaphore_signal(sem, inc=1, device_id=(device,), device_id_type=MESH)

    def tell_line(sem):
        @pl.when(h > 0)
        def _():
            tell(sem, device_of(h - 1, m))

        @pl.when(h < groups - 1)
        def _():
            tell(sem, device_of(h + 1, m))

    beside = jnp.where(h > 0, 1, 0) + jnp.where(h < groups - 1, 1, 0)

    tell(barrier, partner)
    tell_line(barrier)
    each(1, g, lambda s: tell(barrier, device_of(h, across(s))))
    idx_ref[...] = jnp.zeros_like(idx_ref)
    idx_ref[0:kcount, 0:t_dev] = index_ref[...]
    small[...] = jnp.zeros_like(small)
    small[0:1, 0 : cells // 2] = mask_ref[...].astype(f32)
    zmsg[...] = jnp.zeros_like(zmsg)
    pl.semaphore_wait(barrier, g + beside)

    each(1, g, lambda s: idx_copy(s).start())
    load.wait()
    for piece in range(groups):
        own_copy(piece).start()
        each(1, g, lambda s, piece=piece: raw_copy(piece, s).start())
    for turn in range(groups - 2):
        tell_line(round_sem.at[turn])
        pl.semaphore_wait(round_sem.at[turn], beside)
    idx_all[core * g + m] = idx_ref[...]
    each(1, g, lambda s: idx_copy(s).wait())
    relay_copy().start()
    relay_copy().wait()

    def sum_body(at, carry):
        first, second = carry
        value = idx_all[at]
        return first + value, second + value * value

    zero = jnp.zeros((kcount, lanes), f32)
    first, second = lax.fori_loop(0, 2 * g, sum_body, (zero, zero))
    first = jnp.sum(first, 1, keepdims=True)
    second = jnp.sum(second, 1, keepdims=True)
    lane = lax.broadcasted_iota(jnp.int32, (kcount, 128), 1)
    zmsg[0:kcount, :] = jnp.where(lane < 64, first, second)
    ending = pltpu.roll(idx_all[2 * g - 1], (64 - (t_dev - 64)) % lanes, 1)
    zmsg[16 : 16 + kcount, :] = jnp.where(lane < 64, idx_all[0][:, :128], ending[:, :128])
    each(1, groups, lambda s: z_copy(s).start())
    each(1, groups, lambda s: z_copy(s).wait())
    for s in range(1, groups):
        stats = zin[s, 0:kcount, :]
        first = first + stats[:, 0:1]
        second = second + stats[:, 64:65]
    mean = first / total_days
    var = second / total_days - mean * mean
    outer = 1.0 / jnp.sqrt(var + 1e-06)

    place = lax.broadcasted_iota(jnp.int32, (kcount, lanes), 1)

    def centered(value, valid):
        value = (value - mean).astype(jnp.bfloat16).astype(f32)
        return jnp.where(valid, value, 0.0)

    def center_body(at, carry):
        value = centered(idx_all[at], place < t_dev)
        idx_all[at] = value
        return carry + value

    group_sum = jnp.sum(lax.fori_loop(0, 2 * g, center_body, zero), 1, keepdims=True)
    tail = jnp.zeros((kcount, lanes - 128), f32)

    def edge(slot):
        return jnp.concatenate([zin[slot, 16 : 16 + kcount, :], tail], 1)

    before_at, after_at = 2 * g, 2 * g + 1
    ahead = pltpu.roll(edge(1), t_dev - 128, 1)
    idx_all[before_at] = centered(
        ahead, (place >= t_dev - 64) & (place < t_dev) & (h > 0)
    )
    idx_all[after_at] = centered(edge(groups - 1), (place < 64) & (h < groups - 1))

    def slot_at(order):
        inside = lax.rem(order, 2) * g + lax.div(order, 2)
        inside = jnp.where(order < 0, before_at, inside)
        return jnp.where(order >= 2 * g, after_at, inside)

    spot = lax.broadcasted_iota(jnp.int32, (kcount, wide), 1)
    wing = jnp.zeros((kcount, 128), f32)

    def window_body(step, carry):
        order = across(step) * 2 + core
        here = jnp.concatenate([idx_all[slot_at(order)], wing], 1)
        before = jnp.concatenate([idx_all[slot_at(order - 1)], wing], 1)
        after = jnp.concatenate([idx_all[slot_at(order + 1)], wing], 1)
        left = pltpu.roll(before, (REACH - t_dev) % wide, 1)
        mid = pltpu.roll(here, REACH, 1)
        right = pltpu.roll(after, REACH + t_dev, 1)
        ext = jnp.where(spot < REACH, left, jnp.where(spot < REACH + t_dev, mid, right))
        for k in range(kcount):
            line = pltpu.roll(ext[k : k + 1], wide - REACH - MAXLAG + offset_ref[k], 1)
            line = jnp.broadcast_to(line, (ROWS, wide))
            turned = pltpu.roll(line, 0, 1, stride=1, stride_axis=0)
            win[step, k * ROWS : (k + 1) * ROWS, :] = turned[:, :lanes].astype(jnp.bfloat16)
        return carry

    lax.fori_loop(0, g, window_body, 0)

    day = lax.broadcasted_iota(jnp.int32, (lanes, 128), 0)
    shift = lax.broadcasted_iota(jnp.int32, (lanes, 128), 1) - MAXLAG
    late = jnp.where((day >= t_dev - shift) & (day < t_dev), 1.0, 0.0).astype(jnp.bfloat16)
    early = jnp.where(day < -shift, 1.0, 0.0).astype(jnp.bfloat16)

    def part(at, sel):
        return jnp.dot(idx_all[at].astype(jnp.bfloat16), sel, preferred_element_type=f32)

    by_shift = group_sum + (part(before_at, late) - part(2 * g - 1, late)) + (
        part(after_at, early) - part(0, early)
    )
    tot_ref[...] = jnp.zeros_like(tot_ref)
    for k in range(kcount):
        tot_ref[k : k + 1, :] = pltpu.roll(
            by_shift[k : k + 1], lax.rem(128 - offset_ref[k], 128), 1
        )
    own_tot = tot_ref[...]
    own_cols = jnp.transpose(own_tot)

    low = lax.broadcasted_iota(jnp.int32, (ROWS, 128), 1) < 64
    low_row = lax.broadcasted_iota(jnp.int32, (1, 128), 1) < 64

    def pair_cols(cols, k):
        return jnp.where(low, cols[0:ROWS, k : k + 1], cols[0:ROWS, k + half_k : k + half_k + 1])

    def halves(first_half, second_half, is_low):
        turned_first = pltpu.roll(first_half, 64, 1)
        turned_second = pltpu.roll(second_half, 64, 1)
        zeroth = jnp.where(is_low, first_half, turned_second)
        oneth = jnp.where(is_low, turned_first, second_half)
        mine = jnp.where(core == 0, zeroth, oneth)
        theirs = jnp.where(core == 0, oneth, zeroth)
        return mine, theirs

    group_days = 2 * g * t_dev * 1.0
    mine_at = acc.shape[0] - EXTRA

    def products(piece):
        own_copy(piece).wait()

        def add(step, first_time):
            value = recv[piece, step]
            wide_value = value.astype(f32)
            sums = jnp.sum(wide_value, 0, keepdims=True)
            squares = jnp.sum(wide_value * wide_value, 0, keepdims=True)
            found = jnp.dot(win[step, :, :t_dev], value, preferred_element_type=f32)
            if first_time:
                acc[0 : 2 * count, :] = found
                acc[mine_at : mine_at + 1, :] = sums
                acc[mine_at + 1 : mine_at + 2, :] = squares
            else:
                acc[0 : 2 * count, :] += found
                acc[mine_at : mine_at + 1, :] += sums
                acc[mine_at + 1 : mine_at + 2, :] += squares

        add(0, True)

        def body(step, carry):
            raw_copy(piece, step).wait()
            add(step, False)
            return carry

        lax.fori_loop(1, g, body, 0)
        for k in range(half_k):
            at = k * ROWS
            mine, theirs = halves(
                acc[at : at + ROWS, :], acc[count + at : count + at + ROWS, :], low
            )
            acc[at : at + ROWS, :] = mine
            other[piece, at : at + ROWS, :] = theirs
        for row in range(2):
            value = acc[mine_at + row : mine_at + row + 1, :]
            mine, theirs = halves(value, value, low_row)
            acc[mine_at + row : mine_at + row + 1, :] = mine
            other[piece, count + row : count + row + 1, :] = theirs
        swap_copy(piece).start()
        swap_copy(piece).wait()

    def joined(piece, k):
        at = k * ROWS
        return acc[at : at + ROWS, :] + partner_in[piece, at : at + ROWS, :]

    def joined_row(piece, row):
        return (
            acc[mine_at + row : mine_at + row + 1, :]
            + partner_in[piece, count + row : count + row + 1, :]
        )

    other[...] = jnp.zeros_like(other)
    sent_extra[...] = jnp.zeros_like(sent_extra)
    for piece in range(groups - 1):
        products(piece)
        sx = joined_row(piece, 0)
        sent_extra[piece, 0:1, :] = sx
        sent_extra[piece, 1:2, :] = joined_row(piece, 1)
        local_mean = sx / group_days
        for k in range(half_k):
            value = joined(piece, k) - local_mean * pair_cols(own_cols, k)
            top = jnp.max(jnp.abs(value), 0, keepdims=True)
            sent_extra[piece, 2 + k : 3 + k, :] = top
            scaled = value * (TOP / jnp.maximum(top, 1e-30))
            sent[piece, k * ROWS : (k + 1) * ROWS, :] = (
                jnp.round(scaled).astype(jnp.int32).astype(jnp.int16)
            )
        sent_extra[piece, EXTRA:, :] = own_tot
        sum_copy(piece).start()
        extra_copy(piece).start()

    last = groups - 1
    products(last)
    sx = joined_row(last, 0)
    sq = joined_row(last, 1)
    for piece in range(groups - 1):
        extra_copy(piece).wait()
        sum_copy(piece).wait()
        sx = sx + got_extra[piece, 0:1, :]
        sq = sq + got_extra[piece, 1:2, :]
    mean_x = sx / total_days
    var_x = sq / total_days - mean_x * mean_x
    mask = small[0:1, :]
    mask = mask + pltpu.roll(mask, 64, 1)
    inner = mask / (total_days * jnp.sqrt(var_x + 1e-06))
    far_cols = [
        jnp.transpose(got_extra[piece, EXTRA : EXTRA + 16, :]) for piece in range(groups - 1)
    ]
    far_mean = [
        got_extra[piece, 0:1, :] / group_days - mean_x for piece in range(groups - 1)
    ]
    small_int = lag_ref[...] + MAXLAG

    def normal(k):
        value = joined(last, k) - mean_x * pair_cols(own_cols, k)
        for piece in range(groups - 1):
            coded = got[piece, k * ROWS : (k + 1) * ROWS, :].astype(jnp.int32).astype(f32)
            value = value + coded * (got_extra[piece, 2 + k : 3 + k, :] * (1.0 / TOP))
            value = value + far_mean[piece] * pair_cols(far_cols[piece], k)
        scale = jnp.where(low_row, outer[k : k + 1], outer[k + half_k : k + half_k + 1])
        return value * (inner * scale)

    small[0:1, 0 : lag_ref.shape[1]] = small_int.astype(f32)
    chosen = jnp.broadcast_to(small[0:1, :].astype(jnp.int32), (64, 128))
    kept = lag_ref.shape[1]
    for k in range(0, half_k, 2):
        upper = normal(k)
        under = normal(k + 1) if k + 1 < half_k else upper
        flat = jnp.transpose(jnp.concatenate([upper, under], 0))
        for side in range(2):
            rows = flat[side * 64 : (side + 1) * 64, :]
            out_ref[k + side * half_k] = jnp.take_along_axis(rows, chosen, axis=1)[:, :kept]
            if k + 1 < half_k:
                out_ref[k + 1 + side * half_k] = jnp.take_along_axis(
                    rows, chosen + 64, axis=1
                )[:, :kept]


def shards(field, index, lag_list, index_offset, sea_mask):
    t_dev, cells_all = field.shape
    devices = lax.axis_size("tm")
    kcount = index.shape[1]
    lanes = round_up(t_dev, 128)
    groups = GROUPS
    g = devices // 2 // groups
    rows = kcount * ROWS
    half = rows // 2
    sizes = (devices, t_dev, kcount, groups, g)
    dma = pltpu.SemaphoreType.DMA
    f32 = jnp.float32
    vmem = pl.BlockSpec(memory_space=pltpu.VMEM)
    maps = pl.pallas_call(
        functools.partial(kernel, sizes),
        out_shape=jax.ShapeDtypeStruct((kcount, 64, lag_list.shape[0]), f32),
        in_specs=[
            pl.BlockSpec(memory_space=pl.ANY),
            vmem,
            vmem,
            pl.BlockSpec(memory_space=pltpu.SMEM),
            vmem,
        ],
        out_specs=vmem,
        scratch_shapes=[
            pltpu.VMEM((t_dev, cells_all), jnp.bfloat16),
            pltpu.VMEM((kcount, lanes), f32),
            pltpu.VMEM((2 * g + 2, kcount, lanes), f32),
            pltpu.VMEM((32, 128), f32),
            pltpu.VMEM((groups, 32, 128), f32),
            pltpu.VMEM((groups, g, t_dev, 128), jnp.bfloat16),
            pltpu.VMEM((g, rows, lanes), jnp.bfloat16),
            pltpu.VMEM((rows + EXTRA, 128), f32),
            pltpu.VMEM((groups, half + EXTRA, 128), f32),
            pltpu.VMEM((groups, half + EXTRA, 128), f32),
            pltpu.VMEM((groups, half, 128), jnp.int16),
            pltpu.VMEM((groups, EXTRA + 16, 128), f32),
            pltpu.VMEM((groups, half, 128), jnp.int16),
            pltpu.VMEM((groups, EXTRA + 16, 128), f32),
            pltpu.VMEM((8, 128), f32),
            pltpu.VMEM((16, 128), f32),
            dma((groups, g)),
            dma((groups, g)),
            dma((g,)),
            dma((g,)),
            dma((2,)),
            dma((groups,)),
            dma((groups,)),
            dma((groups,)),
            dma((groups,)),
            dma((2, groups)),
            dma((2, groups)),
            dma((groups + 1,)),
            pltpu.SemaphoreType.REGULAR((groups,)),
        ],
        compiler_params=pltpu.CompilerParams(
            collective_id=0, has_side_effects=True, vmem_limit_bytes=60 * 1024 * 1024
        ),
    )(field, index.T, lag_list[None, :], index_offset, sea_mask[None, :])
    return jnp.transpose(maps, (1, 0, 2))


def solution(mesh):
    return jax.shard_map(
        shards,
        mesh=mesh,
        in_specs=(P("tm", None), P("tm", None), P(), P(), P("tm")),
        out_specs=P("tm", None, None),
        check_vma=False,
    )
```

time: 44.2 us -> 35.8 us (0.81)
  the two profiles are of different devices: /device:TPU:9 before, /device:TPU:0 now
where the time goes in v1:
time: 35.8 us; the launch traced here: 35.6 us
  Pallas kernels  33.9 us (95%)
  local copies, waits for them, and re-layouts  1.72 us (5%)
    pallas_call x1, Pallas kernels, shards(): pl.pallas_call(functools.partial(kernel, sizes), out_shape=jax.ShapeDtype...  33.9 us
    unnamed x1, local copies, waits for them, and re-layouts  1.72 us

profile of v1, /device:TPU:0, one launch (start us, length us, event | category | flops | bytes accessed | tf_op | source)
XLA Modules:
  0.0 35.6 jit_solution(17972654397799600378)
XLA Ops:
  0.0 33.9 %shard_map.55 = f32[10,64,61]{2,1,0:T(8,128)} custom-call(bf16[336,2048]{1,0:T(8,128)(2,1)} %field_hbm.1, f32[10,336]{1,0:T(8,128)} %bitcast.5, s32[1,61]{1,0:T(1,128)} %bitcast.6, s32[10]{0:T(128)} %offset_ref.1, s32[1,64]{1,0:T(1,128)} %bitcast.7), custom_call_target="tpu_custom_call" | custom-call | tf_op jit(solution)/shard_map/pallas_call | solution.py:456
  33.9 1.7 %copy.7 = f32[64,10,61]{2,0,1:T(8,128)} copy(f32[64,10,61]{2,0,1:T(8,128)} %bitcast.4) | data formatting | bytes 312320

commit v2 on v1

--- a/solution.py
+++ b/solution.py
@@ -13,6 +13,8 @@
 ROWS = 64
 EXTRA = 8
 TOP = 32767.0
+FAR = 1e30
+NEAR = 1e29
 GROUPS = 4
 MESH = pl.DeviceIdType.MESH
 
@@ -32,9 +34,11 @@
     field_ref,
     idx_ref,
     idx_all,
+    tiles,
     zmsg,
     zin,
     recv,
+    raw_win,
     win,
     acc,
     other,
@@ -43,13 +47,17 @@
     sent_extra,
     got,
     got_extra,
+    far,
     small,
-    tot_ref,
+    tot_part,
+    tot_in,
     raw_send,
     raw_recv,
     idx_send,
     idx_recv,
-    relay_sem,
+    tile_send,
+    tile_recv,
+    lone_sem,
     z_send,
     z_recv,
     swap_send,
@@ -71,15 +79,20 @@
     h = lax.div(chip, g)
     m = lax.rem(chip, g)
     partner = chip * 2 + (1 - core)
+    edge_peer = ((h + 2 * core - 1) * g + m) * 2 + (1 - core)
+    has_edge = jnp.where(core == 0, h > 0, h < groups - 1)
     f32 = jnp.float32
     total_days = devices * t_dev * 1.0
 
+    def flipped(value, step, size):
+        found, bit = 0, 1
+        while bit < size:
+            flip = lax.rem(lax.div(value, bit) + lax.div(step, bit), 2)
+            found, bit = found + flip * bit, bit * 2
+        return found
+
     def across(step):
-        other_m, bit = 0, 1
-        while bit < g:
-            flip = lax.rem(lax.div(m, bit) + lax.div(step, bit), 2)
-            other_m, bit = other_m + flip * bit, bit * 2
-        return other_m
+        return flipped(m, step, g)
 
     def device_of(group, member):
         return (group * g + member) * 2 + core
@@ -98,7 +111,7 @@
         return field_ref.at[:, pl.ds(pl.multiple_of(at * cells, cells), cells)]
 
     def plane_of(piece):
-        return lax.rem(h + 1 + piece, groups)
+        return flipped(h, groups - 1 - piece, groups)
 
     def raw_copy(piece, step):
         to = across(step)
@@ -118,15 +131,30 @@
     def idx_copy(step):
         return remote(
             idx_ref,
-            idx_all.at[core * g + m],
+            idx_all.at[m],
             idx_send.at[step],
             idx_recv.at[step],
             device_of(h, across(step)),
         )
 
-    def relay_copy():
-        part = idx_all.at[pl.ds(core * g, g)]
-        return remote(part, part, relay_sem.at[0], relay_sem.at[1], partner)
+    def tile_copy(side, step):
+        to = (h * g + across(step)) * 2 + (core if side == 0 else 1 - core)
+        mine = tiles.at[core * g + m]
+        return remote(
+            mine, mine, tile_send.at[side, step], tile_recv.at[side, step], to
+        )
+
+    def edge_copy():
+        return remote(
+            tiles.at[jnp.where(core == 0, 0, 2 * g - 1)],
+            tiles.at[2 * g],
+            lone_sem.at[0],
+            lone_sem.at[1],
+            edge_peer,
+        )
+
+    def total_copy():
+        return remote(tot_part, tot_in, lone_sem.at[2], lone_sem.at[3], partner)
 
     def z_copy(step):
         return remote(
@@ -134,7 +162,7 @@
             zin.at[step],
             z_send.at[step],
             z_recv.at[step],
-            device_of(lax.rem(h + step, groups), m),
+            device_of(flipped(h, step, groups), m),
         )
 
     def swap_copy(piece):
@@ -188,17 +216,35 @@
             tell(sem, device_of(h + 1, m))
 
     beside = jnp.where(h > 0, 1, 0) + jnp.where(h < groups - 1, 1, 0)
-
-    tell(barrier, partner)
     tell_line(barrier)
-    each(1, g, lambda s: tell(barrier, device_of(h, across(s))))
+
+    @pl.when(has_edge)
+    def _():
+        tell(barrier, edge_peer)
+
+    each(1, 2 * g, lambda s: tell(barrier, (h * g + across(lax.div(s, 2))) * 2 + lax.rem(core + s, 2)))
     idx_ref[...] = jnp.zeros_like(idx_ref)
     idx_ref[0:kcount, 0:t_dev] = index_ref[...]
+    lane = lax.broadcasted_iota(jnp.int32, (kcount, 128), 1)
+    series = idx_ref[...]
+    tile = jnp.where(
+        lane < 64, series[:, :128], pltpu.roll(series, (128 - t_dev) % lanes, 1)[:, :128]
+    )
+    tile = jnp.where(lane == 62, jnp.sum(series, 1, keepdims=True), tile)
+    tile = jnp.where(lane == 63, jnp.sum(series * series, 1, keepdims=True), tile)
+    tiles[core * g + m] = tile
+    idx_all[m] = series
     small[...] = jnp.zeros_like(small)
     small[0:1, 0 : cells // 2] = mask_ref[...].astype(f32)
-    zmsg[...] = jnp.zeros_like(zmsg)
-    pl.semaphore_wait(barrier, g + beside)
-
+
+    @pl.when(jnp.logical_not(has_edge))
+    def _():
+        tiles[2 * g] = jnp.full((kcount, 128), FAR, f32)
+
+    pl.semaphore_wait(barrier, 2 * g - 1 + beside + jnp.where(has_edge, 1, 0))
+
+    for side in range(2):
+        each(1 - side, g, lambda s, side=side: tile_copy(side, s).start())
     each(1, g, lambda s: idx_copy(s).start())
     load.wait()
     for piece in range(groups):
@@ -207,72 +253,34 @@
     for turn in range(groups - 2):
         tell_line(round_sem.at[turn])
         pl.semaphore_wait(round_sem.at[turn], beside)
-    idx_all[core * g + m] = idx_ref[...]
+    for side in range(2):
+        each(1 - side, g, lambda s, side=side: tile_copy(side, s).wait())
+
+    @pl.when(has_edge)
+    def _():
+        edge_copy().start()
+
+    zero_tile = jnp.zeros((kcount, 128), f32)
+    zmsg[...] = lax.fori_loop(0, 2 * g, lambda at, carry: carry + tiles[at], zero_tile)
+    each(1, groups, lambda s: z_copy(s).start())
     each(1, g, lambda s: idx_copy(s).wait())
-    relay_copy().start()
-    relay_copy().wait()
-
-    def sum_body(at, carry):
-        first, second = carry
-        value = idx_all[at]
-        return first + value, second + value * value
-
-    zero = jnp.zeros((kcount, lanes), f32)
-    first, second = lax.fori_loop(0, 2 * g, sum_body, (zero, zero))
-    first = jnp.sum(first, 1, keepdims=True)
-    second = jnp.sum(second, 1, keepdims=True)
-    lane = lax.broadcasted_iota(jnp.int32, (kcount, 128), 1)
-    zmsg[0:kcount, :] = jnp.where(lane < 64, first, second)
-    ending = pltpu.roll(idx_all[2 * g - 1], (64 - (t_dev - 64)) % lanes, 1)
-    zmsg[16 : 16 + kcount, :] = jnp.where(lane < 64, idx_all[0][:, :128], ending[:, :128])
-    each(1, groups, lambda s: z_copy(s).start())
-    each(1, groups, lambda s: z_copy(s).wait())
-    for s in range(1, groups):
-        stats = zin[s, 0:kcount, :]
-        first = first + stats[:, 0:1]
-        second = second + stats[:, 64:65]
-    mean = first / total_days
-    var = second / total_days - mean * mean
-    outer = 1.0 / jnp.sqrt(var + 1e-06)
-
-    place = lax.broadcasted_iota(jnp.int32, (kcount, lanes), 1)
-
-    def centered(value, valid):
-        value = (value - mean).astype(jnp.bfloat16).astype(f32)
-        return jnp.where(valid, value, 0.0)
-
-    def center_body(at, carry):
-        value = centered(idx_all[at], place < t_dev)
-        idx_all[at] = value
-        return carry + value
-
-    group_sum = jnp.sum(lax.fori_loop(0, 2 * g, center_body, zero), 1, keepdims=True)
-    tail = jnp.zeros((kcount, lanes - 128), f32)
-
-    def edge(slot):
-        return jnp.concatenate([zin[slot, 16 : 16 + kcount, :], tail], 1)
-
-    before_at, after_at = 2 * g, 2 * g + 1
-    ahead = pltpu.roll(edge(1), t_dev - 128, 1)
-    idx_all[before_at] = centered(
-        ahead, (place >= t_dev - 64) & (place < t_dev) & (h > 0)
-    )
-    idx_all[after_at] = centered(edge(groups - 1), (place < 64) & (h < groups - 1))
-
-    def slot_at(order):
-        inside = lax.rem(order, 2) * g + lax.div(order, 2)
-        inside = jnp.where(order < 0, before_at, inside)
-        return jnp.where(order >= 2 * g, after_at, inside)
 
     spot = lax.broadcasted_iota(jnp.int32, (kcount, wide), 1)
     wing = jnp.zeros((kcount, 128), f32)
-
-    def window_body(step, carry):
-        order = across(step) * 2 + core
-        here = jnp.concatenate([idx_all[slot_at(order)], wing], 1)
-        before = jnp.concatenate([idx_all[slot_at(order - 1)], wing], 1)
-        after = jnp.concatenate([idx_all[slot_at(order + 1)], wing], 1)
-        left = pltpu.roll(before, (REACH - t_dev) % wide, 1)
+    tail = jnp.zeros((kcount, wide - 128), f32)
+
+    def tile_at(order):
+        inside = lax.rem(order, 2) * g + lax.div(order, 2)
+        outside = jnp.logical_or(order < 0, order >= 2 * g)
+        return tiles[jnp.where(outside, 2 * g, inside)]
+
+    def window(member):
+        order = member * 2 + core
+        step = flipped(m, member, g)
+        here = jnp.concatenate([idx_all[member], wing], 1)
+        before = jnp.concatenate([tile_at(order - 1), tail], 1)
+        after = jnp.concatenate([tile_at(order + 1), tail], 1)
+        left = pltpu.roll(before, wide - REACH, 1)
         mid = pltpu.roll(here, REACH, 1)
         right = pltpu.roll(after, REACH + t_dev, 1)
         ext = jnp.where(spot < REACH, left, jnp.where(spot < REACH + t_dev, mid, right))
@@ -280,29 +288,67 @@
             line = pltpu.roll(ext[k : k + 1], wide - REACH - MAXLAG + offset_ref[k], 1)
             line = jnp.broadcast_to(line, (ROWS, wide))
             turned = pltpu.roll(line, 0, 1, stride=1, stride_axis=0)
-            win[step, k * ROWS : (k + 1) * ROWS, :] = turned[:, :lanes].astype(jnp.bfloat16)
-        return carry
-
-    lax.fori_loop(0, g, window_body, 0)
-
+            raw_win[step, k * ROWS : (k + 1) * ROWS, :] = turned[:, :lanes]
+
+    each(0, g - 1, lambda at: window(jnp.where(core == 0, g - 1 - at, at)))
+
+    @pl.when(has_edge)
+    def _():
+        edge_copy().wait()
+
+    window(jnp.where(core == 0, 0, g - 1))
+    each(1, groups, lambda s: z_copy(s).wait())
+    stats = zmsg[...]
+    for s in range(1, groups):
+        stats = stats + zin[s]
+    mean = stats[:, 62:63] / total_days
+    var = stats[:, 63:64] / total_days - mean * mean
+    outer = 1.0 / jnp.sqrt(var + 1e-06)
+
+    def center_window(step):
+        for k in range(kcount):
+            value = raw_win[step, k * ROWS : (k + 1) * ROWS, :]
+            value = jnp.where(value < NEAR, value - mean[k : k + 1], 0.0)
+            win[step, k * ROWS : (k + 1) * ROWS, :] = value.astype(jnp.bfloat16)
+
+    each(0, g, center_window)
+
+    place = lax.broadcasted_iota(jnp.int32, (kcount, lanes), 1)
     day = lax.broadcasted_iota(jnp.int32, (lanes, 128), 0)
     shift = lax.broadcasted_iota(jnp.int32, (lanes, 128), 1) - MAXLAG
-    late = jnp.where((day >= t_dev - shift) & (day < t_dev), 1.0, 0.0).astype(jnp.bfloat16)
-    early = jnp.where(day < -shift, 1.0, 0.0).astype(jnp.bfloat16)
-
-    def part(at, sel):
-        return jnp.dot(idx_all[at].astype(jnp.bfloat16), sel, preferred_element_type=f32)
-
-    by_shift = group_sum + (part(before_at, late) - part(2 * g - 1, late)) + (
-        part(after_at, early) - part(0, early)
+    late = jnp.where((day >= t_dev - shift) & (day < t_dev), 1.0, 0.0)
+    early = jnp.where(day < -shift, 1.0, 0.0)
+
+    def centered(value, valid):
+        return jnp.where(valid, (value - mean).astype(jnp.bfloat16).astype(f32), 0.0)
+
+    def center_body(at, carry):
+        return carry + centered(idx_all[at], place < t_dev)
+
+    core_sum = lax.fori_loop(0, g, center_body, jnp.zeros((kcount, lanes), f32))
+    inner_block = centered(idx_all[jnp.where(core == 0, 0, g - 1)], place < t_dev)
+    edge = jnp.concatenate([tiles[2 * g], tail[:, : lanes - 128]], 1)
+    edge = jnp.where(core == 0, pltpu.roll(edge, t_dev - 128, 1), edge)
+    opens = jnp.where(core == 0, t_dev - 64, 0)
+    closes = jnp.where(core == 0, t_dev, 62)
+    outer_block = centered(edge, (place >= opens) & (place < closes) & (edge < NEAR))
+
+    def part(value, sel):
+        return jnp.dot(
+            value.astype(jnp.bfloat16), sel.astype(jnp.bfloat16), preferred_element_type=f32
+        )
+
+    by_shift = (
+        jnp.sum(core_sum, 1, keepdims=True)
+        + part(outer_block, jnp.where(core == 0, late, early))
+        - part(inner_block, jnp.where(core == 0, early, late))
     )
-    tot_ref[...] = jnp.zeros_like(tot_ref)
+    tot_part[...] = jnp.zeros_like(tot_part)
     for k in range(kcount):
-        tot_ref[k : k + 1, :] = pltpu.roll(
+        tot_part[k : k + 1, :] = pltpu.roll(
             by_shift[k : k + 1], lax.rem(128 - offset_ref[k], 128), 1
         )
-    own_tot = tot_ref[...]
-    own_cols = jnp.transpose(own_tot)
+    total_copy().start()
 
     low = lax.broadcasted_iota(jnp.int32, (ROWS, 128), 1) < 64
     low_row = lax.broadcasted_iota(jnp.int32, (1, 128), 1) < 64
@@ -374,9 +420,14 @@
         )
 
     other[...] = jnp.zeros_like(other)
+    far[...] = jnp.zeros_like(far)
     sent_extra[...] = jnp.zeros_like(sent_extra)
     for piece in range(groups - 1):
         products(piece)
+        if piece == 0:
+            total_copy().wait()
+            own_tot = tot_part[...] + tot_in[...]
+            own_cols = jnp.transpose(own_tot)
         sx = joined_row(piece, 0)
         sent_extra[piece, 0:1, :] = sx
         sent_extra[piece, 1:2, :] = joined_row(piece, 1)
@@ -397,33 +448,35 @@
     products(last)
     sx = joined_row(last, 0)
     sq = joined_row(last, 1)
+    all_cols = own_cols
     for piece in range(groups - 1):
         extra_copy(piece).wait()
         sum_copy(piece).wait()
-        sx = sx + got_extra[piece, 0:1, :]
+        far_x = got_extra[piece, 0:1, :]
+        sx = sx + far_x
         sq = sq + got_extra[piece, 1:2, :]
+        far_mean = far_x / group_days
+        far_cols = jnp.transpose(got_extra[piece, EXTRA:, :])
+        all_cols = all_cols + far_cols
+        for k in range(half_k):
+            at = k * ROWS
+            coded = got[piece, at : at + ROWS, :].astype(jnp.int32).astype(f32)
+            far[at : at + ROWS, :] += coded * (
+                got_extra[piece, 2 + k : 3 + k, :] * (1.0 / TOP)
+            ) + far_mean * pair_cols(far_cols, k)
     mean_x = sx / total_days
     var_x = sq / total_days - mean_x * mean_x
     mask = small[0:1, :]
     mask = mask + pltpu.roll(mask, 64, 1)
     inner = mask / (total_days * jnp.sqrt(var_x + 1e-06))
-    far_cols = [
-        jnp.transpose(got_extra[piece, EXTRA : EXTRA + 16, :]) for piece in range(groups - 1)
-    ]
-    far_mean = [
-        got_extra[piece, 0:1, :] / group_days - mean_x for piece in range(groups - 1)
-    ]
-    small_int = lag_ref[...] + MAXLAG
 
     def normal(k):
-        value = joined(last, k) - mean_x * pair_cols(own_cols, k)
-        for piece in range(groups - 1):
-            coded = got[piece, k * ROWS : (k + 1) * ROWS, :].astype(jnp.int32).astype(f32)
-            value = value + coded * (got_extra[piece, 2 + k : 3 + k, :] * (1.0 / TOP))
-            value = value + far_mean[piece] * pair_cols(far_cols[piece], k)
+        value = joined(last, k) + far[k * ROWS : (k + 1) * ROWS, :]
+        value = value - mean_x * pair_cols(all_cols, k)
         scale = jnp.where(low_row, outer[k : k + 1], outer[k + half_k : k + half_k + 1])
         return value * (inner * scale)
 
+    small_int = lag_ref[...] + MAXLAG
     small[0:1, 0 : lag_ref.shape[1]] = small_int.astype(f32)
     chosen = jnp.broadcast_to(small[0:1, :].astype(jnp.int32), (64, 128))
     kept = lag_ref.shape[1]
@@ -467,10 +520,12 @@
         scratch_shapes=[
             pltpu.VMEM((t_dev, cells_all), jnp.bfloat16),
             pltpu.VMEM((kcount, lanes), f32),
-            pltpu.VMEM((2 * g + 2, kcount, lanes), f32),
-            pltpu.VMEM((32, 128), f32),
-            pltpu.VMEM((groups, 32, 128), f32),
+            pltpu.VMEM((g, kcount, lanes), f32),
+            pltpu.VMEM((2 * g + 1, kcount, 128), f32),
+            pltpu.VMEM((kcount, 128), f32),
+            pltpu.VMEM((groups, kcount, 128), f32),
             pltpu.VMEM((groups, g, t_dev, 128), jnp.bfloat16),
+            pltpu.VMEM((g, rows, lanes), f32),
             pltpu.VMEM((g, rows, lanes), jnp.bfloat16),
             pltpu.VMEM((rows + EXTRA, 128), f32),
             pltpu.VMEM((groups, half + EXTRA, 128), f32),
@@ -479,13 +534,17 @@
             pltpu.VMEM((groups, EXTRA + 16, 128), f32),
             pltpu.VMEM((groups, half, 128), jnp.int16),
             pltpu.VMEM((groups, EXTRA + 16, 128), f32),
+            pltpu.VMEM((half, 128), f32),
             pltpu.VMEM((8, 128), f32),
+            pltpu.VMEM((16, 128), f32),
             pltpu.VMEM((16, 128), f32),
             dma((groups, g)),
             dma((groups, g)),
             dma((g,)),
             dma((g,)),
-            dma((2,)),
+            dma((2, g)),
+            dma((2, g)),
+            dma((4,)),
             dma((groups,)),
             dma((groups,)),
             dma((groups,)),

time: 35.8 us -> 34.1 us (0.953)
  Pallas kernels: 33.9 us -> 32.2 us
    pallas_call x1, Pallas kernels: 33.9 us -> 32.2 us  [shards(): pl.pallas_call(functools.partial(kernel, sizes), out_shape=jax.ShapeDtype...]
where the time goes in v2:
time: 34.1 us; the launch traced here: 33.9 us
  Pallas kernels  32.2 us (94%)
  local copies, waits for them, and re-layouts  1.72 us (5%)
    pallas_call x1, Pallas kernels, shards(): pl.pallas_call(functools.partial(kernel, sizes), out_shape=jax.ShapeDtype...  32.2 us
    unnamed x1, local copies, waits for them, and re-layouts  1.72 us

profile of v2, /device:TPU:0, one launch (start us, length us, event | category | flops | bytes accessed | tf_op | source)
XLA Modules:
  0.0 33.9 jit_solution(11558509427930336162)
XLA Ops:
  0.0 32.2 %shard_map.55 = f32[10,64,61]{2,1,0:T(8,128)} custom-call(bf16[336,2048]{1,0:T(8,128)(2,1)} %field_hbm.1, f32[10,336]{1,0:T(8,128)} %bitcast.5, s32[1,61]{1,0:T(1,128)} %bitcast.6, s32[10]{0:T(128)} %offset_ref.1, s32[1,64]{1,0:T(1,128)} %bitcast.7), custom_call_target="tpu_custom_call" | custom-call | tf_op jit(solution)/shard_map/pallas_call | solution.py:509
  32.2 1.7 %copy.7 = f32[64,10,61]{2,0,1:T(8,128)} copy(f32[64,10,61]{2,0,1:T(8,128)} %bitcast.4) | data formatting | bytes 312320

commit v3 on v2

--- a/solution.py
+++ b/solution.py
@@ -11,6 +11,7 @@
 MAXOFF = 14
 REACH = 64
 ROWS = 64
+BASE = 16
 EXTRA = 8
 TOP = 32767.0
 FAR = 1e30
@@ -41,6 +42,7 @@
     raw_win,
     win,
     acc,
+    mine,
     other,
     partner_in,
     sent,
@@ -139,9 +141,9 @@
 
     def tile_copy(side, step):
         to = (h * g + across(step)) * 2 + (core if side == 0 else 1 - core)
-        mine = tiles.at[core * g + m]
-        return remote(
-            mine, mine, tile_send.at[side, step], tile_recv.at[side, step], to
+        tile = tiles.at[core * g + m]
+        return remote(
+            tile, tile, tile_send.at[side, step], tile_recv.at[side, step], to
         )
 
     def edge_copy():
@@ -234,6 +236,9 @@
     tile = jnp.where(lane == 63, jnp.sum(series * series, 1, keepdims=True), tile)
     tiles[core * g + m] = tile
     idx_all[m] = series
+    other[...] = jnp.zeros_like(other)
+    far[...] = jnp.zeros_like(far)
+    sent_extra[...] = jnp.zeros_like(sent_extra)
     small[...] = jnp.zeros_like(small)
     small[0:1, 0 : cells // 2] = mask_ref[...].astype(f32)
 
@@ -286,9 +291,10 @@
         ext = jnp.where(spot < REACH, left, jnp.where(spot < REACH + t_dev, mid, right))
         for k in range(kcount):
             line = pltpu.roll(ext[k : k + 1], wide - REACH - MAXLAG + offset_ref[k], 1)
-            line = jnp.broadcast_to(line, (ROWS, wide))
-            turned = pltpu.roll(line, 0, 1, stride=1, stride_axis=0)
-            raw_win[step, k * ROWS : (k + 1) * ROWS, :] = turned[:, :lanes]
+            line = jnp.broadcast_to(line, (BASE, wide))
+            raw_win[step, k * BASE : (k + 1) * BASE, :] = pltpu.roll(
+                line, 0, 1, stride=1, stride_axis=0
+            )
 
     each(0, g - 1, lambda at: window(jnp.where(core == 0, g - 1 - at, at)))
 
@@ -307,48 +313,11 @@
 
     def center_window(step):
         for k in range(kcount):
-            value = raw_win[step, k * ROWS : (k + 1) * ROWS, :]
-            value = jnp.where(value < NEAR, value - mean[k : k + 1], 0.0)
-            win[step, k * ROWS : (k + 1) * ROWS, :] = value.astype(jnp.bfloat16)
-
-    each(0, g, center_window)
-
-    place = lax.broadcasted_iota(jnp.int32, (kcount, lanes), 1)
-    day = lax.broadcasted_iota(jnp.int32, (lanes, 128), 0)
-    shift = lax.broadcasted_iota(jnp.int32, (lanes, 128), 1) - MAXLAG
-    late = jnp.where((day >= t_dev - shift) & (day < t_dev), 1.0, 0.0)
-    early = jnp.where(day < -shift, 1.0, 0.0)
-
-    def centered(value, valid):
-        return jnp.where(valid, (value - mean).astype(jnp.bfloat16).astype(f32), 0.0)
-
-    def center_body(at, carry):
-        return carry + centered(idx_all[at], place < t_dev)
-
-    core_sum = lax.fori_loop(0, g, center_body, jnp.zeros((kcount, lanes), f32))
-    inner_block = centered(idx_all[jnp.where(core == 0, 0, g - 1)], place < t_dev)
-    edge = jnp.concatenate([tiles[2 * g], tail[:, : lanes - 128]], 1)
-    edge = jnp.where(core == 0, pltpu.roll(edge, t_dev - 128, 1), edge)
-    opens = jnp.where(core == 0, t_dev - 64, 0)
-    closes = jnp.where(core == 0, t_dev, 62)
-    outer_block = centered(edge, (place >= opens) & (place < closes) & (edge < NEAR))
-
-    def part(value, sel):
-        return jnp.dot(
-            value.astype(jnp.bfloat16), sel.astype(jnp.bfloat16), preferred_element_type=f32
-        )
-
-    by_shift = (
-        jnp.sum(core_sum, 1, keepdims=True)
-        + part(outer_block, jnp.where(core == 0, late, early))
-        - part(inner_block, jnp.where(core == 0, early, late))
-    )
-    tot_part[...] = jnp.zeros_like(tot_part)
-    for k in range(kcount):
-        tot_part[k : k + 1, :] = pltpu.roll(
-            by_shift[k : k + 1], lax.rem(128 - offset_ref[k], 128), 1
-        )
-    total_copy().start()
+            value = raw_win[step, k * BASE : (k + 1) * BASE, :]
+            value = jnp.where(value < NEAR, value - mean[k : k + 1], 0.0).astype(jnp.bfloat16)
+            for turn in range(0, ROWS, BASE):
+                turned = value if turn == 0 else pltpu.roll(value, turn, 1)
+                win[step, k * ROWS + turn : k * ROWS + turn + BASE, :] = turned[:, :lanes]
 
     low = lax.broadcasted_iota(jnp.int32, (ROWS, 128), 1) < 64
     low_row = lax.broadcasted_iota(jnp.int32, (1, 128), 1) < 64
@@ -361,73 +330,65 @@
         turned_second = pltpu.roll(second_half, 64, 1)
         zeroth = jnp.where(is_low, first_half, turned_second)
         oneth = jnp.where(is_low, turned_first, second_half)
-        mine = jnp.where(core == 0, zeroth, oneth)
-        theirs = jnp.where(core == 0, oneth, zeroth)
-        return mine, theirs
+        return jnp.where(core == 0, zeroth, oneth), jnp.where(core == 0, oneth, zeroth)
 
     group_days = 2 * g * t_dev * 1.0
-    mine_at = acc.shape[0] - EXTRA
+    sums_at = 2 * count
+
+    def add(pieces, step, first_time):
+        width = 128 * len(pieces)
+        value = jnp.concatenate([recv[piece, step] for piece in pieces], 1)
+        wide_value = value.astype(f32)
+        sums = jnp.sum(wide_value, 0, keepdims=True)
+        squares = jnp.sum(wide_value * wide_value, 0, keepdims=True)
+        found = jnp.dot(win[step, :, :t_dev], value, preferred_element_type=f32)
+        if first_time:
+            acc[0:sums_at, :width] = found
+            acc[sums_at : sums_at + 1, :width] = sums
+            acc[sums_at + 1 : sums_at + 2, :width] = squares
+        else:
+            acc[0:sums_at, :width] += found
+            acc[sums_at : sums_at + 1, :width] += sums
+            acc[sums_at + 1 : sums_at + 2, :width] += squares
+
+    def split(piece, column):
+        column = slice(column * 128, column * 128 + 128)
+        for k in range(half_k):
+            at = k * ROWS
+            kept, given = halves(
+                acc[at : at + ROWS, column], acc[count + at : count + at + ROWS, column], low
+            )
+            mine[piece, at : at + ROWS, :] = kept
+            other[piece, at : at + ROWS, :] = given
+        for row in range(2):
+            value = acc[sums_at + row : sums_at + row + 1, column]
+            kept, given = halves(value, value, low_row)
+            mine[piece, count + row : count + row + 1, :] = kept
+            other[piece, count + row : count + row + 1, :] = given
+        swap_copy(piece).start()
 
     def products(piece):
         own_copy(piece).wait()
-
-        def add(step, first_time):
-            value = recv[piece, step]
-            wide_value = value.astype(f32)
-            sums = jnp.sum(wide_value, 0, keepdims=True)
-            squares = jnp.sum(wide_value * wide_value, 0, keepdims=True)
-            found = jnp.dot(win[step, :, :t_dev], value, preferred_element_type=f32)
-            if first_time:
-                acc[0 : 2 * count, :] = found
-                acc[mine_at : mine_at + 1, :] = sums
-                acc[mine_at + 1 : mine_at + 2, :] = squares
-            else:
-                acc[0 : 2 * count, :] += found
-                acc[mine_at : mine_at + 1, :] += sums
-                acc[mine_at + 1 : mine_at + 2, :] += squares
-
-        add(0, True)
+        add([piece], 0, True)
 
         def body(step, carry):
             raw_copy(piece, step).wait()
-            add(step, False)
+            add([piece], step, False)
             return carry
 
         lax.fori_loop(1, g, body, 0)
-        for k in range(half_k):
-            at = k * ROWS
-            mine, theirs = halves(
-                acc[at : at + ROWS, :], acc[count + at : count + at + ROWS, :], low
-            )
-            acc[at : at + ROWS, :] = mine
-            other[piece, at : at + ROWS, :] = theirs
-        for row in range(2):
-            value = acc[mine_at + row : mine_at + row + 1, :]
-            mine, theirs = halves(value, value, low_row)
-            acc[mine_at + row : mine_at + row + 1, :] = mine
-            other[piece, count + row : count + row + 1, :] = theirs
-        swap_copy(piece).start()
-        swap_copy(piece).wait()
+        split(piece, 0)
 
     def joined(piece, k):
         at = k * ROWS
-        return acc[at : at + ROWS, :] + partner_in[piece, at : at + ROWS, :]
+        return mine[piece, at : at + ROWS, :] + partner_in[piece, at : at + ROWS, :]
 
     def joined_row(piece, row):
-        return (
-            acc[mine_at + row : mine_at + row + 1, :]
-            + partner_in[piece, count + row : count + row + 1, :]
-        )
-
-    other[...] = jnp.zeros_like(other)
-    far[...] = jnp.zeros_like(far)
-    sent_extra[...] = jnp.zeros_like(sent_extra)
-    for piece in range(groups - 1):
-        products(piece)
-        if piece == 0:
-            total_copy().wait()
-            own_tot = tot_part[...] + tot_in[...]
-            own_cols = jnp.transpose(own_tot)
+        at = count + row
+        return mine[piece, at : at + 1, :] + partner_in[piece, at : at + 1, :]
+
+    def send_sums(piece):
+        swap_copy(piece).wait()
         sx = joined_row(piece, 0)
         sent_extra[piece, 0:1, :] = sx
         sent_extra[piece, 1:2, :] = joined_row(piece, 1)
@@ -445,9 +406,72 @@
         extra_copy(piece).start()
 
     last = groups - 1
+    early_pieces = [0, 1] if last > 1 else [0]
+    for piece in early_pieces:
+        own_copy(piece).wait()
+        each(1, g, lambda s, piece=piece: raw_copy(piece, s).wait())
+
+    def early_body(step, first_time):
+        center_window(step)
+        add(early_pieces, step, first_time)
+
+    early_body(0, True)
+    if g <= 4:
+        for step in range(1, g):
+            early_body(step, False)
+    else:
+        each(1, g, lambda s: early_body(s, False))
+    for piece in early_pieces:
+        split(piece, piece)
+
+    place = lax.broadcasted_iota(jnp.int32, (kcount, lanes), 1)
+    day = lax.broadcasted_iota(jnp.int32, (lanes, 128), 0)
+    shift = lax.broadcasted_iota(jnp.int32, (lanes, 128), 1) - MAXLAG
+    late = jnp.where((day >= t_dev - shift) & (day < t_dev), 1.0, 0.0)
+    early = jnp.where(day < -shift, 1.0, 0.0)
+
+    def centered(value, valid):
+        return jnp.where(valid, (value - mean).astype(jnp.bfloat16).astype(f32), 0.0)
+
+    def center_body(at, carry):
+        return carry + centered(idx_all[at], place < t_dev)
+
+    core_sum = lax.fori_loop(0, g, center_body, jnp.zeros((kcount, lanes), f32))
+    inner_block = centered(idx_all[jnp.where(core == 0, 0, g - 1)], place < t_dev)
+    edge = jnp.concatenate([tiles[2 * g], tail[:, : lanes - 128]], 1)
+    edge = jnp.where(core == 0, pltpu.roll(edge, t_dev - 128, 1), edge)
+    opens = jnp.where(core == 0, t_dev - 64, 0)
+    closes = jnp.where(core == 0, t_dev, 62)
+    outer_block = centered(edge, (place >= opens) & (place < closes) & (edge < NEAR))
+
+    def part(value, sel):
+        return jnp.dot(
+            value.astype(jnp.bfloat16), sel.astype(jnp.bfloat16), preferred_element_type=f32
+        )
+
+    by_shift = (
+        jnp.sum(core_sum, 1, keepdims=True)
+        + part(outer_block, jnp.where(core == 0, late, early))
+        - part(inner_block, jnp.where(core == 0, early, late))
+    )
+    tot_part[...] = jnp.zeros_like(tot_part)
+    for k in range(kcount):
+        tot_part[k : k + 1, :] = pltpu.roll(
+            by_shift[k : k + 1], lax.rem(128 - offset_ref[k], 128), 1
+        )
+    total_copy().start()
+
+    total_copy().wait()
+    own_tot = tot_part[...] + tot_in[...]
+    own_cols = jnp.transpose(own_tot)
+    for piece in early_pieces:
+        send_sums(piece)
+    for piece in range(len(early_pieces), last):
+        products(piece)
+        send_sums(piece)
     products(last)
-    sx = joined_row(last, 0)
-    sq = joined_row(last, 1)
+    sx = jnp.zeros((1, 128), f32)
+    sq = jnp.zeros((1, 128), f32)
     all_cols = own_cols
     for piece in range(groups - 1):
         extra_copy(piece).wait()
@@ -464,6 +488,9 @@
             far[at : at + ROWS, :] += coded * (
                 got_extra[piece, 2 + k : 3 + k, :] * (1.0 / TOP)
             ) + far_mean * pair_cols(far_cols, k)
+    swap_copy(last).wait()
+    sx = sx + joined_row(last, 0)
+    sq = sq + joined_row(last, 1)
     mean_x = sx / total_days
     var_x = sq / total_days - mean_x * mean_x
     mask = small[0:1, :]
@@ -525,9 +552,10 @@
             pltpu.VMEM((kcount, 128), f32),
             pltpu.VMEM((groups, kcount, 128), f32),
             pltpu.VMEM((groups, g, t_dev, 128), jnp.bfloat16),
-            pltpu.VMEM((g, rows, lanes), f32),
+            pltpu.VMEM((g, kcount * BASE, lanes + 128), f32),
             pltpu.VMEM((g, rows, lanes), jnp.bfloat16),
-            pltpu.VMEM((rows + EXTRA, 128), f32),
+            pltpu.VMEM((rows + EXTRA, 256), f32),
+            pltpu.VMEM((groups, half + EXTRA, 128), f32),
             pltpu.VMEM((groups, half + EXTRA, 128), f32),
             pltpu.VMEM((groups, half + EXTRA, 128), f32),
             pltpu.VMEM((groups, half, 128), jnp.int16),

time: 34.1 us -> 36.4 us (1.067)
  Pallas kernels: 32.2 us -> 34.4 us
    pallas_call x1, Pallas kernels: 32.2 us -> 34.4 us  [shards(): pl.pallas_call(functools.partial(kernel, sizes), out_shape=jax.ShapeDtype...]
where the time goes in v3:
time: 36.4 us; the launch traced here: 36.1 us
  Pallas kernels  34.4 us (95%)
  local copies, waits for them, and re-layouts  1.72 us (5%)
    pallas_call x1, Pallas kernels, shards(): pl.pallas_call(functools.partial(kernel, sizes), out_shape=jax.ShapeDtype...  34.4 us
    unnamed x1, local copies, waits for them, and re-layouts  1.72 us

profile of v3, /device:TPU:0, one launch (start us, length us, event | category | flops | bytes accessed | tf_op | source)
XLA Modules:
  0.0 36.1 jit_solution(1034409668614710450)
XLA Ops:
  0.0 34.4 %shard_map.55 = f32[10,64,61]{2,1,0:T(8,128)} custom-call(bf16[336,2048]{1,0:T(8,128)(2,1)} %field_hbm.1, f32[10,336]{1,0:T(8,128)} %bitcast.5, s32[1,61]{1,0:T(1,128)} %bitcast.6, s32[10]{0:T(128)} %offset_ref.1, s32[1,64]{1,0:T(1,128)} %bitcast.7), custom_call_target="tpu_custom_call" | custom-call | tf_op jit(solution)/shard_map/pallas_call | solution.py:536
  34.4 1.7 %copy.7 = f32[64,10,61]{2,0,1:T(8,128)} copy(f32[64,10,61]{2,0,1:T(8,128)} %bitcast.4) | data formatting | bytes 312320

commit v4 on v3

--- a/solution.py
+++ b/solution.py
@@ -50,6 +50,7 @@
     got,
     got_extra,
     far,
+    out_buf,
     small,
     tot_part,
     tot_in,
@@ -68,6 +69,7 @@
     sum_recv,
     own_sem,
     round_sem,
+    out_sem,
 ):
     devices, t_dev, kcount, groups, g = sizes
     lanes = idx_ref.shape[1]
@@ -112,8 +114,16 @@
     def block(at):
         return field_ref.at[:, pl.ds(pl.multiple_of(at * cells, cells), cells)]
 
+    inner = jnp.logical_or(h == 1, h == 2)
+    upper = lax.div(h, 2)
+    beside_h = h + 1 - 2 * lax.rem(h, 2)
+
     def plane_of(piece):
-        return flipped(h, groups - 1 - piece, groups)
+        if piece == 0:
+            return (groups - 1) * (1 - upper)
+        if piece == 1:
+            return 2 - upper
+        return beside_h if piece == 2 else h
 
     def raw_copy(piece, step):
         to = across(step)
@@ -176,23 +186,35 @@
             partner,
         )
 
-    def sum_copy(piece):
-        return remote(
-            sent.at[piece],
-            got.at[piece],
-            sum_send.at[0, piece],
-            sum_recv.at[0, piece],
-            device_of(plane_of(piece), m),
-        )
-
-    def extra_copy(piece):
-        return remote(
-            sent_extra.at[piece],
-            got_extra.at[piece],
-            sum_send.at[1, piece],
-            sum_recv.at[1, piece],
-            device_of(plane_of(piece), m),
-        )
+    def slot_of(piece):
+        return piece if piece == 2 else jnp.where(inner, 3, piece)
+
+    def receiver(piece):
+        if piece == 2:
+            return device_of(beside_h, m)
+        return device_of(jnp.where(inner, plane_of(piece), beside_h), m)
+
+    def sum_copies(piece, slot):
+        return [
+            remote(
+                sent.at[piece],
+                got.at[slot],
+                sum_send.at[0, piece],
+                sum_recv.at[0, slot],
+                receiver(piece),
+            ),
+            remote(
+                sent_extra.at[piece],
+                got_extra.at[slot],
+                sum_send.at[1, piece],
+                sum_recv.at[1, slot],
+                receiver(piece),
+            ),
+        ]
+
+    def arrived(slot):
+        for copy in sum_copies(2, slot):
+            copy.wait_recv()
 
     def each(low_step, high_step, act):
         def body(step, carry):
@@ -387,33 +409,55 @@
         at = count + row
         return mine[piece, at : at + 1, :] + partner_in[piece, at : at + 1, :]
 
-    def send_sums(piece):
-        swap_copy(piece).wait()
-        sx = joined_row(piece, 0)
+    def decoded(slot, k):
+        coded = got[slot, k * ROWS : (k + 1) * ROWS, :].astype(jnp.int32).astype(f32)
+        return coded * (got_extra[slot, 2 + k : 3 + k, :] * (1.0 / TOP))
+
+    def send_sums(piece, with_outer):
+        sx, sq = joined_row(piece, 0), joined_row(piece, 1)
+        tot, cols, days = own_tot, own_cols, group_days
+        if with_outer:
+            arrived(piece)
+            outer_x = got_extra[piece, 0:1, :]
+            outer_mean = outer_x / group_days
+            sx, sq = sx + outer_x, sq + got_extra[piece, 1:2, :]
+            outer_tot = got_extra[piece, EXTRA:, :]
+            outer_cols = jnp.transpose(outer_tot)
+            tot, cols, days = tot + outer_tot, cols + outer_cols, 2 * group_days
         sent_extra[piece, 0:1, :] = sx
-        sent_extra[piece, 1:2, :] = joined_row(piece, 1)
-        local_mean = sx / group_days
+        sent_extra[piece, 1:2, :] = sq
+        local_mean = sx / days
         for k in range(half_k):
-            value = joined(piece, k) - local_mean * pair_cols(own_cols, k)
+            value = joined(piece, k) - local_mean * pair_cols(cols, k)
+            if with_outer:
+                value = value + decoded(piece, k) + outer_mean * pair_cols(outer_cols, k)
             top = jnp.max(jnp.abs(value), 0, keepdims=True)
             sent_extra[piece, 2 + k : 3 + k, :] = top
             scaled = value * (TOP / jnp.maximum(top, 1e-30))
             sent[piece, k * ROWS : (k + 1) * ROWS, :] = (
                 jnp.round(scaled).astype(jnp.int32).astype(jnp.int16)
             )
-        sent_extra[piece, EXTRA:, :] = own_tot
-        sum_copy(piece).start()
-        extra_copy(piece).start()
+        sent_extra[piece, EXTRA:, :] = tot
+        for copy in sum_copies(piece, slot_of(piece)):
+            copy.start()
+
+    def send_outer(piece):
+        @pl.when(jnp.logical_not(inner))
+        def _():
+            send_sums(piece, False)
+
+    def send_inner(piece):
+        @pl.when(inner)
+        def _():
+            send_sums(piece, True)
 
     last = groups - 1
-    early_pieces = [0, 1] if last > 1 else [0]
-    for piece in early_pieces:
-        own_copy(piece).wait()
-        each(1, g, lambda s, piece=piece: raw_copy(piece, s).wait())
+    own_copy(0).wait()
+    each(1, g, lambda s: raw_copy(0, s).wait())
 
     def early_body(step, first_time):
         center_window(step)
-        add(early_pieces, step, first_time)
+        add([0], step, first_time)
 
     early_body(0, True)
     if g <= 4:
@@ -421,8 +465,7 @@
             early_body(step, False)
     else:
         each(1, g, lambda s: early_body(s, False))
-    for piece in early_pieces:
-        split(piece, piece)
+    split(0, 0)
 
     place = lax.broadcasted_iota(jnp.int32, (kcount, lanes), 1)
     day = lax.broadcasted_iota(jnp.int32, (lanes, 128), 0)
@@ -464,30 +507,34 @@
     total_copy().wait()
     own_tot = tot_part[...] + tot_in[...]
     own_cols = jnp.transpose(own_tot)
-    for piece in early_pieces:
-        send_sums(piece)
-    for piece in range(len(early_pieces), last):
-        products(piece)
-        send_sums(piece)
+    swap_copy(0).wait()
+    send_outer(0)
+    products(1)
+    swap_copy(1).wait()
+    send_outer(1)
+    send_inner(0)
+    products(2)
+    swap_copy(2).wait()
+    send_sums(2, False)
+    send_inner(1)
     products(last)
     sx = jnp.zeros((1, 128), f32)
     sq = jnp.zeros((1, 128), f32)
     all_cols = own_cols
-    for piece in range(groups - 1):
-        extra_copy(piece).wait()
-        sum_copy(piece).wait()
-        far_x = got_extra[piece, 0:1, :]
+    for slot, days in ((3, 2 * group_days), (2, group_days)):
+        arrived(slot)
+        far_x = got_extra[slot, 0:1, :]
         sx = sx + far_x
-        sq = sq + got_extra[piece, 1:2, :]
-        far_mean = far_x / group_days
-        far_cols = jnp.transpose(got_extra[piece, EXTRA:, :])
+        sq = sq + got_extra[slot, 1:2, :]
+        far_mean = far_x / days
+        far_cols = jnp.transpose(got_extra[slot, EXTRA:, :])
         all_cols = all_cols + far_cols
         for k in range(half_k):
             at = k * ROWS
-            coded = got[piece, at : at + ROWS, :].astype(jnp.int32).astype(f32)
-            far[at : at + ROWS, :] += coded * (
-                got_extra[piece, 2 + k : 3 + k, :] * (1.0 / TOP)
-            ) + far_mean * pair_cols(far_cols, k)
+            far[at : at + ROWS, :] += decoded(slot, k) + far_mean * pair_cols(far_cols, k)
+    for piece in range(last):
+        for copy in sum_copies(piece, slot_of(piece)):
+            copy.wait_send()
     swap_copy(last).wait()
     sx = sx + joined_row(last, 0)
     sq = sq + joined_row(last, 1)
@@ -507,17 +554,22 @@
     small[0:1, 0 : lag_ref.shape[1]] = small_int.astype(f32)
     chosen = jnp.broadcast_to(small[0:1, :].astype(jnp.int32), (64, 128))
     kept = lag_ref.shape[1]
+
+    def out_copy(k):
+        return pltpu.make_async_copy(out_buf.at[k], out_ref.at[k], out_sem.at[k])
+
     for k in range(0, half_k, 2):
-        upper = normal(k)
-        under = normal(k + 1) if k + 1 < half_k else upper
-        flat = jnp.transpose(jnp.concatenate([upper, under], 0))
+        upper_rows = normal(k)
+        under_rows = normal(k + 1) if k + 1 < half_k else upper_rows
+        flat = jnp.transpose(jnp.concatenate([upper_rows, under_rows], 0))
         for side in range(2):
             rows = flat[side * 64 : (side + 1) * 64, :]
-            out_ref[k + side * half_k] = jnp.take_along_axis(rows, chosen, axis=1)[:, :kept]
-            if k + 1 < half_k:
-                out_ref[k + 1 + side * half_k] = jnp.take_along_axis(
-                    rows, chosen + 64, axis=1
-                )[:, :kept]
+            for turn in range(min(2, half_k - k)):
+                at = k + turn + side * half_k
+                out_buf[at] = jnp.take_along_axis(rows, chosen + 64 * turn, axis=1)[:, :kept]
+                out_copy(at).start()
+    for k in range(kcount):
+        out_copy(k).wait()
 
 
 def shards(field, index, lag_list, index_offset, sea_mask):
@@ -543,7 +595,7 @@
             pl.BlockSpec(memory_space=pltpu.SMEM),
             vmem,
         ],
-        out_specs=vmem,
+        out_specs=pl.BlockSpec(memory_space=pl.ANY),
         scratch_shapes=[
             pltpu.VMEM((t_dev, cells_all), jnp.bfloat16),
             pltpu.VMEM((kcount, lanes), f32),
@@ -563,6 +615,7 @@
             pltpu.VMEM((groups, half, 128), jnp.int16),
             pltpu.VMEM((groups, EXTRA + 16, 128), f32),
             pltpu.VMEM((half, 128), f32),
+            pltpu.VMEM((kcount, 64, lag_list.shape[0]), f32),
             pltpu.VMEM((8, 128), f32),
             pltpu.VMEM((16, 128), f32),
             pltpu.VMEM((16, 128), f32),
@@ -581,6 +634,7 @@
             dma((2, groups)),
             dma((groups + 1,)),
             pltpu.SemaphoreType.REGULAR((groups,)),
+            dma((kcount,)),
         ],
         compiler_params=pltpu.CompilerParams(
             collective_id=0, has_side_effects=True, vmem_limit_bytes=60 * 1024 * 1024

time: 36.4 us -> 31.6 us (0.87)
  Pallas kernels: 34.4 us -> 29.7 us
    pallas_call x1, Pallas kernels: 34.4 us -> 29.7 us  [shards(): pl.pallas_call(functools.partial(kernel, sizes), out_shape=jax.ShapeDtype...]
where the time goes in v4:
time: 31.6 us; the launch traced here: 31.4 us
  Pallas kernels  29.7 us (94%)
  local copies, waits for them, and re-layouts  1.72 us (5%)
    pallas_call x1, Pallas kernels, shards(): pl.pallas_call(functools.partial(kernel, sizes), out_shape=jax.ShapeDtype...  29.7 us
    unnamed x1, local copies, waits for them, and re-layouts  1.72 us

profile of v4, /device:TPU:0, one launch (start us, length us, event | category | flops | bytes accessed | tf_op | source)
XLA Modules:
  0.0 31.4 jit_solution(18176983012583617757)
XLA Ops:
  0.0 29.7 %shard_map.55 = f32[10,64,61]{2,1,0:T(8,128)} custom-call(bf16[336,2048]{1,0:T(8,128)(2,1)} %field_hbm.1, f32[10,336]{1,0:T(8,128)} %bitcast.5, s32[1,61]{1,0:T(1,128)} %bitcast.6, s32[10]{0:T(128)} %offset_ref.1, s32[1,64]{1,0:T(1,128)} %bitcast.7), custom_call_target="tpu_custom_call" | custom-call | tf_op jit(solution)/shard_map/pallas_call | solution.py:588
  29.7 1.7 %copy.7 = f32[64,10,61]{2,0,1:T(8,128)} copy(f32[64,10,61]{2,0,1:T(8,128)} %bitcast.4) | data formatting | bytes 312320

commit v5 on v4

--- a/solution.py
+++ b/solution.py
@@ -122,8 +122,8 @@
         if piece == 0:
             return (groups - 1) * (1 - upper)
         if piece == 1:
-            return 2 - upper
-        return beside_h if piece == 2 else h
+            return jnp.where(inner, beside_h, 2 - upper)
+        return jnp.where(inner, 2 - upper, beside_h) if piece == 2 else h
 
     def raw_copy(piece, step):
         to = across(step)
@@ -187,10 +187,10 @@
         )
 
     def slot_of(piece):
-        return piece if piece == 2 else jnp.where(inner, 3, piece)
+        return jnp.where(inner, (3, 2, 3)[piece], piece)
 
     def receiver(piece):
-        if piece == 2:
+        if piece == 1:
             return device_of(beside_h, m)
         return device_of(jnp.where(inner, plane_of(piece), beside_h), m)
 
@@ -213,7 +213,7 @@
         ]
 
     def arrived(slot):
-        for copy in sum_copies(2, slot):
+        for copy in sum_copies(1, slot):
             copy.wait_recv()
 
     def each(low_step, high_step, act):
@@ -333,6 +333,43 @@
     var = stats[:, 63:64] / total_days - mean * mean
     outer = 1.0 / jnp.sqrt(var + 1e-06)
 
+    place = lax.broadcasted_iota(jnp.int32, (kcount, lanes), 1)
+    day = lax.broadcasted_iota(jnp.int32, (lanes, 128), 0)
+    shift = lax.broadcasted_iota(jnp.int32, (lanes, 128), 1) - MAXLAG
+    late = jnp.where((day >= t_dev - shift) & (day < t_dev), 1.0, 0.0)
+    early = jnp.where(day < -shift, 1.0, 0.0)
+
+    def centered(value, valid):
+        return jnp.where(valid, (value - mean).astype(jnp.bfloat16).astype(f32), 0.0)
+
+    def center_body(at, carry):
+        return carry + centered(idx_all[at], place < t_dev)
+
+    core_sum = lax.fori_loop(0, g, center_body, jnp.zeros((kcount, lanes), f32))
+    inner_block = centered(idx_all[jnp.where(core == 0, 0, g - 1)], place < t_dev)
+    edge = jnp.concatenate([tiles[2 * g], tail[:, : lanes - 128]], 1)
+    edge = jnp.where(core == 0, pltpu.roll(edge, t_dev - 128, 1), edge)
+    opens = jnp.where(core == 0, t_dev - 64, 0)
+    closes = jnp.where(core == 0, t_dev, 62)
+    outer_block = centered(edge, (place >= opens) & (place < closes) & (edge < NEAR))
+
+    def part(value, sel):
+        return jnp.dot(
+            value.astype(jnp.bfloat16), sel.astype(jnp.bfloat16), preferred_element_type=f32
+        )
+
+    by_shift = (
+        jnp.sum(core_sum, 1, keepdims=True)
+        + part(outer_block, jnp.where(core == 0, late, early))
+        - part(inner_block, jnp.where(core == 0, early, late))
+    )
+    tot_part[...] = jnp.zeros_like(tot_part)
+    for k in range(kcount):
+        tot_part[k : k + 1, :] = pltpu.roll(
+            by_shift[k : k + 1], lax.rem(128 - offset_ref[k], 128), 1
+        )
+    total_copy().start()
+
     def center_window(step):
         for k in range(kcount):
             value = raw_win[step, k * BASE : (k + 1) * BASE, :]
@@ -413,15 +450,15 @@
         coded = got[slot, k * ROWS : (k + 1) * ROWS, :].astype(jnp.int32).astype(f32)
         return coded * (got_extra[slot, 2 + k : 3 + k, :] * (1.0 / TOP))
 
-    def send_sums(piece, with_outer):
+    def send_sums(piece, outer_slot):
         sx, sq = joined_row(piece, 0), joined_row(piece, 1)
         tot, cols, days = own_tot, own_cols, group_days
-        if with_outer:
-            arrived(piece)
-            outer_x = got_extra[piece, 0:1, :]
+        if outer_slot is not None:
+            arrived(outer_slot)
+            outer_x = got_extra[outer_slot, 0:1, :]
             outer_mean = outer_x / group_days
-            sx, sq = sx + outer_x, sq + got_extra[piece, 1:2, :]
-            outer_tot = got_extra[piece, EXTRA:, :]
+            sx, sq = sx + outer_x, sq + got_extra[outer_slot, 1:2, :]
+            outer_tot = got_extra[outer_slot, EXTRA:, :]
             outer_cols = jnp.transpose(outer_tot)
             tot, cols, days = tot + outer_tot, cols + outer_cols, 2 * group_days
         sent_extra[piece, 0:1, :] = sx
@@ -429,8 +466,8 @@
         local_mean = sx / days
         for k in range(half_k):
             value = joined(piece, k) - local_mean * pair_cols(cols, k)
-            if with_outer:
-                value = value + decoded(piece, k) + outer_mean * pair_cols(outer_cols, k)
+            if outer_slot is not None:
+                value = value + decoded(outer_slot, k) + outer_mean * pair_cols(outer_cols, k)
             top = jnp.max(jnp.abs(value), 0, keepdims=True)
             sent_extra[piece, 2 + k : 3 + k, :] = top
             scaled = value * (TOP / jnp.maximum(top, 1e-30))
@@ -444,12 +481,12 @@
     def send_outer(piece):
         @pl.when(jnp.logical_not(inner))
         def _():
-            send_sums(piece, False)
-
-    def send_inner(piece):
+            send_sums(piece, None)
+
+    def send_inner(piece, outer_slot):
         @pl.when(inner)
         def _():
-            send_sums(piece, True)
+            send_sums(piece, outer_slot)
 
     last = groups - 1
     own_copy(0).wait()
@@ -467,43 +504,6 @@
         each(1, g, lambda s: early_body(s, False))
     split(0, 0)
 
-    place = lax.broadcasted_iota(jnp.int32, (kcount, lanes), 1)
-    day = lax.broadcasted_iota(jnp.int32, (lanes, 128), 0)
-    shift = lax.broadcasted_iota(jnp.int32, (lanes, 128), 1) - MAXLAG
-    late = jnp.where((day >= t_dev - shift) & (day < t_dev), 1.0, 0.0)
-    early = jnp.where(day < -shift, 1.0, 0.0)
-
-    def centered(value, valid):
-        return jnp.where(valid, (value - mean).astype(jnp.bfloat16).astype(f32), 0.0)
-
-    def center_body(at, carry):
-        return carry + centered(idx_all[at], place < t_dev)
-
-    core_sum = lax.fori_loop(0, g, center_body, jnp.zeros((kcount, lanes), f32))
-    inner_block = centered(idx_all[jnp.where(core == 0, 0, g - 1)], place < t_dev)
-    edge = jnp.concatenate([tiles[2 * g], tail[:, : lanes - 128]], 1)
-    edge = jnp.where(core == 0, pltpu.roll(edge, t_dev - 128, 1), edge)
-    opens = jnp.where(core == 0, t_dev - 64, 0)
-    closes = jnp.where(core == 0, t_dev, 62)
-    outer_block = centered(edge, (place >= opens) & (place < closes) & (edge < NEAR))
-
-    def part(value, sel):
-        return jnp.dot(
-            value.astype(jnp.bfloat16), sel.astype(jnp.bfloat16), preferred_element_type=f32
-        )
-
-    by_shift = (
-        jnp.sum(core_sum, 1, keepdims=True)
-        + part(outer_block, jnp.where(core == 0, late, early))
-        - part(inner_block, jnp.where(core == 0, early, late))
-    )
-    tot_part[...] = jnp.zeros_like(tot_part)
-    for k in range(kcount):
-        tot_part[k : k + 1, :] = pltpu.roll(
-            by_shift[k : k + 1], lax.rem(128 - offset_ref[k], 128), 1
-        )
-    total_copy().start()
-
     total_copy().wait()
     own_tot = tot_part[...] + tot_in[...]
     own_cols = jnp.transpose(own_tot)
@@ -511,12 +511,12 @@
     send_outer(0)
     products(1)
     swap_copy(1).wait()
-    send_outer(1)
-    send_inner(0)
+    send_sums(1, None)
     products(2)
+    send_inner(0, 0)
     swap_copy(2).wait()
-    send_sums(2, False)
-    send_inner(1)
+    send_outer(2)
+    send_inner(2, 1)
     products(last)
     sx = jnp.zeros((1, 128), f32)
     sq = jnp.zeros((1, 128), f32)

time: 31.6 us -> 31.3 us (level)
  no operation moved by 1% of the time
where the time goes in v5:
time: 31.3 us; the launch traced here: 31.1 us
  Pallas kernels  29.4 us (94%)
  local copies, waits for them, and re-layouts  1.72 us (5%)
    pallas_call x1, Pallas kernels, shards(): pl.pallas_call(functools.partial(kernel, sizes), out_shape=jax.ShapeDtype...  29.4 us
    unnamed x1, local copies, waits for them, and re-layouts  1.72 us

profile of v5, /device:TPU:0, one launch (start us, length us, event | category | flops | bytes accessed | tf_op | source)
XLA Modules:
  0.0 31.1 jit_solution(2132537797418655577)
XLA Ops:
  0.0 29.4 %shard_map.55 = f32[10,64,61]{2,1,0:T(8,128)} custom-call(bf16[336,2048]{1,0:T(8,128)(2,1)} %field_hbm.1, f32[10,336]{1,0:T(8,128)} %bitcast.5, s32[1,61]{1,0:T(1,128)} %bitcast.6, s32[10]{0:T(128)} %offset_ref.1, s32[1,64]{1,0:T(1,128)} %bitcast.7), custom_call_target="tpu_custom_call" | custom-call | tf_op jit(solution)/shard_map/pallas_call | solution.py:588
  29.4 1.7 %copy.7 = f32[64,10,61]{2,0,1:T(8,128)} copy(f32[64,10,61]{2,0,1:T(8,128)} %bitcast.4) | data formatting | bytes 312320

commit v6 on v5

--- a/solution.py
+++ b/solution.py
@@ -50,6 +50,7 @@
     got,
     got_extra,
     far,
+    stage,
     out_buf,
     small,
     tot_part,
@@ -195,26 +196,27 @@
         return device_of(jnp.where(inner, plane_of(piece), beside_h), m)
 
     def sum_copies(piece, slot):
-        return [
-            remote(
-                sent.at[piece],
-                got.at[slot],
-                sum_send.at[0, piece],
-                sum_recv.at[0, slot],
-                receiver(piece),
-            ),
+        copies = [
             remote(
                 sent_extra.at[piece],
                 got_extra.at[slot],
-                sum_send.at[1, piece],
-                sum_recv.at[1, slot],
+                sum_send.at[half_k, piece],
+                sum_recv.at[half_k, slot],
                 receiver(piece),
-            ),
+            )
         ]
-
-    def arrived(slot):
-        for copy in sum_copies(1, slot):
-            copy.wait_recv()
+        for k in range(half_k):
+            rows = pl.ds(k * ROWS, ROWS)
+            copies.append(
+                remote(
+                    sent.at[piece, rows],
+                    got.at[slot, rows],
+                    sum_send.at[k, piece],
+                    sum_recv.at[k, slot],
+                    receiver(piece),
+                )
+            )
+        return copies
 
     def each(low_step, high_step, act):
         def body(step, carry):
@@ -259,7 +261,6 @@
     tiles[core * g + m] = tile
     idx_all[m] = series
     other[...] = jnp.zeros_like(other)
-    far[...] = jnp.zeros_like(far)
     sent_extra[...] = jnp.zeros_like(sent_extra)
     small[...] = jnp.zeros_like(small)
     small[0:1, 0 : cells // 2] = mask_ref[...].astype(f32)
@@ -453,8 +454,10 @@
     def send_sums(piece, outer_slot):
         sx, sq = joined_row(piece, 0), joined_row(piece, 1)
         tot, cols, days = own_tot, own_cols, group_days
+        copies = sum_copies(piece, slot_of(piece))
         if outer_slot is not None:
-            arrived(outer_slot)
+            arriving = sum_copies(1, outer_slot)
+            arriving[0].wait_recv()
             outer_x = got_extra[outer_slot, 0:1, :]
             outer_mean = outer_x / group_days
             sx, sq = sx + outer_x, sq + got_extra[outer_slot, 1:2, :]
@@ -467,16 +470,24 @@
         for k in range(half_k):
             value = joined(piece, k) - local_mean * pair_cols(cols, k)
             if outer_slot is not None:
-                value = value + decoded(outer_slot, k) + outer_mean * pair_cols(outer_cols, k)
+                value = value + outer_mean * pair_cols(outer_cols, k)
+            stage[k * ROWS : (k + 1) * ROWS, :] = value
             top = jnp.max(jnp.abs(value), 0, keepdims=True)
+            if outer_slot is not None:
+                top = top + got_extra[outer_slot, 2 + k : 3 + k, :]
             sent_extra[piece, 2 + k : 3 + k, :] = top
-            scaled = value * (TOP / jnp.maximum(top, 1e-30))
+        sent_extra[piece, EXTRA:, :] = tot
+        copies[0].start()
+        for k in range(half_k):
+            value = stage[k * ROWS : (k + 1) * ROWS, :]
+            if outer_slot is not None:
+                arriving[1 + k].wait_recv()
+                value = value + decoded(outer_slot, k)
+            scaled = value * (TOP / jnp.maximum(sent_extra[piece, 2 + k : 3 + k, :], 1e-30))
             sent[piece, k * ROWS : (k + 1) * ROWS, :] = (
                 jnp.round(scaled).astype(jnp.int32).astype(jnp.int16)
             )
-        sent_extra[piece, EXTRA:, :] = tot
-        for copy in sum_copies(piece, slot_of(piece)):
-            copy.start()
+            copies[1 + k].start()
 
     def send_outer(piece):
         @pl.when(jnp.logical_not(inner))
@@ -512,8 +523,8 @@
     products(1)
     swap_copy(1).wait()
     send_sums(1, None)
+    send_inner(0, 0)
     products(2)
-    send_inner(0, 0)
     swap_copy(2).wait()
     send_outer(2)
     send_inner(2, 1)
@@ -521,8 +532,9 @@
     sx = jnp.zeros((1, 128), f32)
     sq = jnp.zeros((1, 128), f32)
     all_cols = own_cols
-    for slot, days in ((3, 2 * group_days), (2, group_days)):
-        arrived(slot)
+    for slot, days in ((2, group_days), (3, 2 * group_days)):
+        arriving = sum_copies(1, slot)
+        arriving[0].wait_recv()
         far_x = got_extra[slot, 0:1, :]
         sx = sx + far_x
         sq = sq + got_extra[slot, 1:2, :]
@@ -531,7 +543,9 @@
         all_cols = all_cols + far_cols
         for k in range(half_k):
             at = k * ROWS
-            far[at : at + ROWS, :] += decoded(slot, k) + far_mean * pair_cols(far_cols, k)
+            arriving[1 + k].wait_recv()
+            value = decoded(slot, k) + far_mean * pair_cols(far_cols, k)
+            far[at : at + ROWS, :] = value if slot == 2 else far[at : at + ROWS, :] + value
     for piece in range(last):
         for copy in sum_copies(piece, slot_of(piece)):
             copy.wait_send()
@@ -615,6 +629,7 @@
             pltpu.VMEM((groups, half, 128), jnp.int16),
             pltpu.VMEM((groups, EXTRA + 16, 128), f32),
             pltpu.VMEM((half, 128), f32),
+            pltpu.VMEM((half, 128), f32),
             pltpu.VMEM((kcount, 64, lag_list.shape[0]), f32),
             pltpu.VMEM((8, 128), f32),
             pltpu.VMEM((16, 128), f32),
@@ -630,8 +645,8 @@
             dma((groups,)),
             dma((groups,)),
             dma((groups,)),
-            dma((2, groups)),
-            dma((2, groups)),
+            dma((kcount // 2 + 1, groups)),
+            dma((kcount // 2 + 1, groups)),
             dma((groups + 1,)),
             pltpu.SemaphoreType.REGULAR((groups,)),
             dma((kcount,)),

time: 31.3 us -> 30.3 us (0.968)
  Pallas kernels: 29.4 us -> 28.3 us
    pallas_call x1, Pallas kernels: 29.4 us -> 28.3 us  [shards(): pl.pallas_call(functools.partial(kernel, sizes), out_shape=jax.ShapeDtype...]
where the time goes in v6:
time: 30.3 us; the launch traced here: 30.1 us
  Pallas kernels  28.3 us (93%)
  local copies, waits for them, and re-layouts  1.72 us (6%)
    pallas_call x1, Pallas kernels, shards(): pl.pallas_call(functools.partial(kernel, sizes), out_shape=jax.ShapeDtype...  28.3 us
    unnamed x1, local copies, waits for them, and re-layouts  1.72 us

profile of v6, /device:TPU:0, one launch (start us, length us, event | category | flops | bytes accessed | tf_op | source)
XLA Modules:
  0.0 30.1 jit_solution(13174176585455986940)
XLA Ops:
  0.0 28.3 %shard_map.55 = f32[10,64,61]{2,1,0:T(8,128)} custom-call(bf16[336,2048]{1,0:T(8,128)(2,1)} %field_hbm.1, f32[10,336]{1,0:T(8,128)} %bitcast.5, s32[1,61]{1,0:T(1,128)} %bitcast.6, s32[10]{0:T(128)} %offset_ref.1, s32[1,64]{1,0:T(1,128)} %bitcast.7), custom_call_target="tpu_custom_call" | custom-call | tf_op jit(solution)/shard_map/pallas_call | solution.py:602
  28.3 1.7 %copy.7 = f32[64,10,61]{2,0,1:T(8,128)} copy(f32[64,10,61]{2,0,1:T(8,128)} %bitcast.4) | data formatting | bytes 312320

commit v7 on v6

--- a/solution.py
+++ b/solution.py
@@ -27,11 +27,15 @@
 def kernel(
     sizes,
     field_hbm,
+    index_hbm,
+    lag_hbm,
+    offset_hbm,
+    mask_hbm,
+    out_ref,
     index_ref,
     lag_ref,
     offset_ref,
     mask_ref,
-    out_ref,
     field_ref,
     idx_ref,
     idx_all,
@@ -71,6 +75,7 @@
     own_sem,
     round_sem,
     out_sem,
+    in_sem,
 ):
     devices, t_dev, kcount, groups, g = sizes
     lanes = idx_ref.shape[1]
@@ -131,8 +136,8 @@
         return remote(
             block(plane_of(piece) * g + to),
             recv.at[piece, step],
-            raw_send.at[piece, step],
-            raw_recv.at[piece, step],
+            raw_send.at[piece],
+            raw_recv.at[piece, step - 1],
             device_of(h, to),
         )
 
@@ -145,8 +150,8 @@
         return remote(
             idx_ref,
             idx_all.at[m],
-            idx_send.at[step],
-            idx_recv.at[step],
+            idx_send.at[0],
+            idx_recv.at[step - 1],
             device_of(h, across(step)),
         )
 
@@ -154,7 +159,7 @@
         to = (h * g + across(step)) * 2 + (core if side == 0 else 1 - core)
         tile = tiles.at[core * g + m]
         return remote(
-            tile, tile, tile_send.at[side, step], tile_recv.at[side, step], to
+            tile, tile, tile_send.at[0], tile_recv.at[side * g + step - 1], to
         )
 
     def edge_copy():
@@ -173,17 +178,18 @@
         return remote(
             zmsg,
             zin.at[step],
-            z_send.at[step],
-            z_recv.at[step],
+            z_send.at[0],
+            z_recv.at[step - 1],
             device_of(flipped(h, step, groups), m),
         )
 
-    def swap_copy(piece):
+    def swap_copy(piece, k):
+        rows = pl.ds(k * ROWS, ROWS if k < half_k else EXTRA)
         return remote(
-            other.at[piece],
-            partner_in.at[piece],
+            other.at[piece, rows],
+            partner_in.at[piece, rows],
             swap_send.at[piece],
-            swap_recv.at[piece],
+            swap_recv.at[piece, k],
             partner,
         )
 
@@ -200,7 +206,7 @@
             remote(
                 sent_extra.at[piece],
                 got_extra.at[slot],
-                sum_send.at[half_k, piece],
+                sum_send.at[1, piece],
                 sum_recv.at[half_k, slot],
                 receiver(piece),
             )
@@ -211,7 +217,7 @@
                 remote(
                     sent.at[piece, rows],
                     got.at[slot, rows],
-                    sum_send.at[k, piece],
+                    sum_send.at[0, piece],
                     sum_recv.at[k, slot],
                     receiver(piece),
                 )
@@ -226,7 +232,17 @@
         lax.fori_loop(low_step, high_step, body, 0)
 
     load = pltpu.make_async_copy(field_hbm, field_ref, own_sem.at[groups])
-    load.start()
+    inputs = [
+        pltpu.make_async_copy(src, dst, in_sem.at[at])
+        for at, (src, dst) in enumerate(
+            (
+                (index_hbm, index_ref),
+                (lag_hbm, lag_ref),
+                (offset_hbm, offset_ref),
+                (mask_hbm, mask_ref),
+            )
+        )
+    ]
     barrier = pltpu.get_barrier_semaphore()
 
     def tell(sem, device):
@@ -249,7 +265,15 @@
         tell(barrier, edge_peer)
 
     each(1, 2 * g, lambda s: tell(barrier, (h * g + across(lax.div(s, 2))) * 2 + lax.rem(core + s, 2)))
+    inputs[0].start()
+    load.start()
+    for copy in inputs[1:]:
+        copy.start()
     idx_ref[...] = jnp.zeros_like(idx_ref)
+    other[...] = jnp.zeros_like(other)
+    sent_extra[...] = jnp.zeros_like(sent_extra)
+    small[...] = jnp.zeros_like(small)
+    inputs[0].wait()
     idx_ref[0:kcount, 0:t_dev] = index_ref[...]
     lane = lax.broadcasted_iota(jnp.int32, (kcount, 128), 1)
     series = idx_ref[...]
@@ -260,10 +284,6 @@
     tile = jnp.where(lane == 63, jnp.sum(series * series, 1, keepdims=True), tile)
     tiles[core * g + m] = tile
     idx_all[m] = series
-    other[...] = jnp.zeros_like(other)
-    sent_extra[...] = jnp.zeros_like(sent_extra)
-    small[...] = jnp.zeros_like(small)
-    small[0:1, 0 : cells // 2] = mask_ref[...].astype(f32)
 
     @pl.when(jnp.logical_not(has_edge))
     def _():
@@ -275,6 +295,9 @@
         each(1 - side, g, lambda s, side=side: tile_copy(side, s).start())
     each(1, g, lambda s: idx_copy(s).start())
     load.wait()
+    for copy in inputs[1:]:
+        copy.wait()
+    small[0:1, 0 : cells // 2] = mask_ref[...].astype(f32)
     for piece in range(groups):
         own_copy(piece).start()
         each(1, g, lambda s, piece=piece: raw_copy(piece, s).start())
@@ -282,7 +305,7 @@
         tell_line(round_sem.at[turn])
         pl.semaphore_wait(round_sem.at[turn], beside)
     for side in range(2):
-        each(1 - side, g, lambda s, side=side: tile_copy(side, s).wait())
+        each(1 - side, g, lambda s, side=side: tile_copy(side, s).wait_recv())
 
     @pl.when(has_edge)
     def _():
@@ -291,7 +314,7 @@
     zero_tile = jnp.zeros((kcount, 128), f32)
     zmsg[...] = lax.fori_loop(0, 2 * g, lambda at, carry: carry + tiles[at], zero_tile)
     each(1, groups, lambda s: z_copy(s).start())
-    each(1, g, lambda s: idx_copy(s).wait())
+    each(1, g, lambda s: idx_copy(s).wait_recv())
 
     spot = lax.broadcasted_iota(jnp.int32, (kcount, wide), 1)
     wing = jnp.zeros((kcount, 128), f32)
@@ -326,7 +349,7 @@
         edge_copy().wait()
 
     window(jnp.where(core == 0, 0, g - 1))
-    each(1, groups, lambda s: z_copy(s).wait())
+    each(1, groups, lambda s: z_copy(s).wait_recv())
     stats = zmsg[...]
     for s in range(1, groups):
         stats = stats + zin[s]
@@ -413,6 +436,12 @@
 
     def split(piece, column):
         column = slice(column * 128, column * 128 + 128)
+        for row in range(2):
+            value = acc[sums_at + row : sums_at + row + 1, column]
+            kept, given = halves(value, value, low_row)
+            mine[piece, count + row : count + row + 1, :] = kept
+            other[piece, count + row : count + row + 1, :] = given
+        swap_copy(piece, half_k).start()
         for k in range(half_k):
             at = k * ROWS
             kept, given = halves(
@@ -420,19 +449,14 @@
             )
             mine[piece, at : at + ROWS, :] = kept
             other[piece, at : at + ROWS, :] = given
-        for row in range(2):
-            value = acc[sums_at + row : sums_at + row + 1, column]
-            kept, given = halves(value, value, low_row)
-            mine[piece, count + row : count + row + 1, :] = kept
-            other[piece, count + row : count + row + 1, :] = given
-        swap_copy(piece).start()
+            swap_copy(piece, k).start()
 
     def products(piece):
         own_copy(piece).wait()
         add([piece], 0, True)
 
         def body(step, carry):
-            raw_copy(piece, step).wait()
+            raw_copy(piece, step).wait_recv()
             add([piece], step, False)
             return carry
 
@@ -441,6 +465,7 @@
 
     def joined(piece, k):
         at = k * ROWS
+        swap_copy(piece, k).wait_recv()
         return mine[piece, at : at + ROWS, :] + partner_in[piece, at : at + ROWS, :]
 
     def joined_row(piece, row):
@@ -452,6 +477,7 @@
         return coded * (got_extra[slot, 2 + k : 3 + k, :] * (1.0 / TOP))
 
     def send_sums(piece, outer_slot):
+        swap_copy(piece, half_k).wait_recv()
         sx, sq = joined_row(piece, 0), joined_row(piece, 1)
         tot, cols, days = own_tot, own_cols, group_days
         copies = sum_copies(piece, slot_of(piece))
@@ -501,7 +527,7 @@
 
     last = groups - 1
     own_copy(0).wait()
-    each(1, g, lambda s: raw_copy(0, s).wait())
+    each(1, g, lambda s: raw_copy(0, s).wait_recv())
 
     def early_body(step, first_time):
         center_window(step)
@@ -518,14 +544,11 @@
     total_copy().wait()
     own_tot = tot_part[...] + tot_in[...]
     own_cols = jnp.transpose(own_tot)
-    swap_copy(0).wait()
     send_outer(0)
     products(1)
-    swap_copy(1).wait()
     send_sums(1, None)
     send_inner(0, 0)
     products(2)
-    swap_copy(2).wait()
     send_outer(2)
     send_inner(2, 1)
     products(last)
@@ -546,10 +569,7 @@
             arriving[1 + k].wait_recv()
             value = decoded(slot, k) + far_mean * pair_cols(far_cols, k)
             far[at : at + ROWS, :] = value if slot == 2 else far[at : at + ROWS, :] + value
-    for piece in range(last):
-        for copy in sum_copies(piece, slot_of(piece)):
-            copy.wait_send()
-    swap_copy(last).wait()
+    swap_copy(last, half_k).wait_recv()
     sx = sx + joined_row(last, 0)
     sq = sq + joined_row(last, 1)
     mean_x = sx / total_days
@@ -570,7 +590,7 @@
     kept = lag_ref.shape[1]
 
     def out_copy(k):
-        return pltpu.make_async_copy(out_buf.at[k], out_ref.at[k], out_sem.at[k])
+        return pltpu.make_async_copy(out_buf.at[k], out_ref.at[k], out_sem.at[0])
 
     for k in range(0, half_k, 2):
         upper_rows = normal(k)
@@ -582,8 +602,19 @@
                 at = k + turn + side * half_k
                 out_buf[at] = jnp.take_along_axis(rows, chosen + 64 * turn, axis=1)[:, :kept]
                 out_copy(at).start()
-    for k in range(kcount):
-        out_copy(k).wait()
+    def drained(ref, sem):
+        remote(ref, ref, sem, sem, partner).wait_send()
+
+    drained(idx_all.at[pl.ds(0, g - 1)], idx_send.at[0])
+    drained(tiles.at[pl.ds(0, 2 * g - 1)], tile_send.at[0])
+    drained(zin.at[pl.ds(0, groups - 1)], z_send.at[0])
+    for piece in range(groups):
+        drained(recv.at[piece, pl.ds(0, g - 1)], raw_send.at[piece])
+        drained(other.at[piece], swap_send.at[piece])
+        if piece < last:
+            drained(sent.at[piece], sum_send.at[0, piece])
+            drained(sent_extra.at[piece], sum_send.at[1, piece])
+    pltpu.make_async_copy(out_buf, out_ref, out_sem.at[0]).wait()
 
 
 def shards(field, index, lag_list, index_offset, sea_mask):
@@ -598,19 +629,16 @@
     sizes = (devices, t_dev, kcount, groups, g)
     dma = pltpu.SemaphoreType.DMA
     f32 = jnp.float32
-    vmem = pl.BlockSpec(memory_space=pltpu.VMEM)
     maps = pl.pallas_call(
         functools.partial(kernel, sizes),
         out_shape=jax.ShapeDtypeStruct((kcount, 64, lag_list.shape[0]), f32),
-        in_specs=[
-            pl.BlockSpec(memory_space=pl.ANY),
-            vmem,
-            vmem,
-            pl.BlockSpec(memory_space=pltpu.SMEM),
-            vmem,
-        ],
+        in_specs=[pl.BlockSpec(memory_space=pl.ANY)] * 5,
         out_specs=pl.BlockSpec(memory_space=pl.ANY),
         scratch_shapes=[
+            pltpu.VMEM((kcount, t_dev), f32),
+            pltpu.VMEM((1, lag_list.shape[0]), jnp.int32),
+            pltpu.SMEM((kcount,), jnp.int32),
+            pltpu.VMEM((1, sea_mask.shape[0]), jnp.int32),
             pltpu.VMEM((t_dev, cells_all), jnp.bfloat16),
             pltpu.VMEM((kcount, lanes), f32),
             pltpu.VMEM((g, kcount, lanes), f32),
@@ -634,22 +662,23 @@
             pltpu.VMEM((8, 128), f32),
             pltpu.VMEM((16, 128), f32),
             pltpu.VMEM((16, 128), f32),
-            dma((groups, g)),
-            dma((groups, g)),
-            dma((g,)),
-            dma((g,)),
-            dma((2, g)),
-            dma((2, g)),
+            dma((groups,)),
+            dma((groups, g - 1)),
+            dma((1,)),
+            dma((g - 1,)),
+            dma((1,)),
+            dma((2 * g - 1,)),
             dma((4,)),
+            dma((1,)),
+            dma((groups - 1,)),
             dma((groups,)),
-            dma((groups,)),
-            dma((groups,)),
-            dma((groups,)),
-            dma((kcount // 2 + 1, groups)),
+            dma((groups, kcount // 2 + 1)),
+            dma((2, groups - 1)),
             dma((kcount // 2 + 1, groups)),
             dma((groups + 1,)),
-            pltpu.SemaphoreType.REGULAR((groups,)),
-            dma((kcount,)),
+            pltpu.SemaphoreType.REGULAR((groups - 2,)),
+            dma((1,)),
+            dma((4,)),
         ],
         compiler_params=pltpu.CompilerParams(
             collective_id=0, has_side_effects=True, vmem_limit_bytes=60 * 1024 * 1024

time: 30.3 us -> 29.4 us (0.970)
  Pallas kernels: 28.3 us -> 27.2 us
    pallas_call x1, Pallas kernels: 28.3 us -> 27.2 us  [shards(): pl.pallas_call(functools.partial(kernel, sizes), out_shape=jax.ShapeDtype...]
where the time goes in v7:
time: 29.4 us; the launch traced here: 28.9 us
  Pallas kernels  27.2 us (93%)
  local copies, waits for them, and re-layouts  1.72 us (6%)
    pallas_call x1, Pallas kernels, shards(): pl.pallas_call(functools.partial(kernel, sizes), out_shape=jax.ShapeDtype...  27.2 us
    unnamed x1, local copies, waits for them, and re-layouts  1.72 us

profile of v7, /device:TPU:0, one launch (start us, length us, event | category | flops | bytes accessed | tf_op | source)
XLA Modules:
  0.0 28.9 jit_solution(6989529029884950681)
XLA Ops:
  0.0 27.2 %shard_map.55 = f32[10,64,61]{2,1,0:T(8,128)} custom-call(bf16[336,2048]{1,0:T(8,128)(2,1)} %field_hbm.1, f32[10,336]{1,0:T(8,128)} %bitcast.5, s32[1,61]{1,0:T(1,128)} %bitcast.6, s32[10]{0:T(128)} %offset_hbm.1, s32[1,64]{1,0:T(1,128)} %bitcast.7), custom_call_target="tpu_custom_call" | custom-call | tf_op jit(solution)/shard_map/pallas_call | solution.py:632
  27.2 1.7 %copy.7 = f32[64,10,61]{2,0,1:T(8,128)} copy(f32[64,10,61]{2,0,1:T(8,128)} %bitcast.4) | data formatting | bytes 312320

commit v8 on v7

--- a/solution.py
+++ b/solution.py
@@ -55,6 +55,7 @@
     got_extra,
     far,
     stage,
+    chooser,
     out_buf,
     small,
     tot_part,
@@ -349,6 +350,12 @@
         edge_copy().wait()
 
     window(jnp.where(core == 0, 0, g - 1))
+    day = lax.broadcasted_iota(jnp.int32, (lanes, 128), 0)
+    shift = lax.broadcasted_iota(jnp.int32, (lanes, 128), 1) - MAXLAG
+    late = jnp.where((day >= t_dev - shift) & (day < t_dev), 1.0, 0.0)
+    early = jnp.where(day < -shift, 1.0, 0.0)
+    chooser[0] = jnp.where(core == 0, late, early).astype(jnp.bfloat16)
+    chooser[1] = jnp.where(core == 0, early, late).astype(jnp.bfloat16)
     each(1, groups, lambda s: z_copy(s).wait_recv())
     stats = zmsg[...]
     for s in range(1, groups):
@@ -358,10 +365,6 @@
     outer = 1.0 / jnp.sqrt(var + 1e-06)
 
     place = lax.broadcasted_iota(jnp.int32, (kcount, lanes), 1)
-    day = lax.broadcasted_iota(jnp.int32, (lanes, 128), 0)
-    shift = lax.broadcasted_iota(jnp.int32, (lanes, 128), 1) - MAXLAG
-    late = jnp.where((day >= t_dev - shift) & (day < t_dev), 1.0, 0.0)
-    early = jnp.where(day < -shift, 1.0, 0.0)
 
     def centered(value, valid):
         return jnp.where(valid, (value - mean).astype(jnp.bfloat16).astype(f32), 0.0)
@@ -377,15 +380,15 @@
     closes = jnp.where(core == 0, t_dev, 62)
     outer_block = centered(edge, (place >= opens) & (place < closes) & (edge < NEAR))
 
-    def part(value, sel):
+    def part(value, side):
         return jnp.dot(
-            value.astype(jnp.bfloat16), sel.astype(jnp.bfloat16), preferred_element_type=f32
+            value.astype(jnp.bfloat16), chooser[side], preferred_element_type=f32
         )
 
     by_shift = (
         jnp.sum(core_sum, 1, keepdims=True)
-        + part(outer_block, jnp.where(core == 0, late, early))
-        - part(inner_block, jnp.where(core == 0, early, late))
+        + part(outer_block, 0)
+        - part(inner_block, 1)
     )
     tot_part[...] = jnp.zeros_like(tot_part)
     for k in range(kcount):
@@ -552,35 +555,37 @@
     send_outer(2)
     send_inner(2, 1)
     products(last)
-    sx = jnp.zeros((1, 128), f32)
-    sq = jnp.zeros((1, 128), f32)
-    all_cols = own_cols
-    for slot, days in ((2, group_days), (3, 2 * group_days)):
-        arriving = sum_copies(1, slot)
-        arriving[0].wait_recv()
+    near_blocks, far_blocks = sum_copies(1, 2), sum_copies(1, 3)
+
+    def opened(slot, copies, days):
+        copies[0].wait_recv()
         far_x = got_extra[slot, 0:1, :]
-        sx = sx + far_x
-        sq = sq + got_extra[slot, 1:2, :]
-        far_mean = far_x / days
-        far_cols = jnp.transpose(got_extra[slot, EXTRA:, :])
-        all_cols = all_cols + far_cols
-        for k in range(half_k):
-            at = k * ROWS
-            arriving[1 + k].wait_recv()
-            value = decoded(slot, k) + far_mean * pair_cols(far_cols, k)
-            far[at : at + ROWS, :] = value if slot == 2 else far[at : at + ROWS, :] + value
+        cols = jnp.transpose(got_extra[slot, EXTRA:, :])
+        return far_x, got_extra[slot, 1:2, :], far_x / days, cols
+
+    near_x, near_sq, near_mean, near_cols = opened(2, near_blocks, group_days)
+    for k in range(half_k):
+        near_blocks[1 + k].wait_recv()
+        far[k * ROWS : (k + 1) * ROWS, :] = decoded(2, k) + near_mean * pair_cols(near_cols, k)
     swap_copy(last, half_k).wait_recv()
-    sx = sx + joined_row(last, 0)
-    sq = sq + joined_row(last, 1)
-    mean_x = sx / total_days
-    var_x = sq / total_days - mean_x * mean_x
+    far_x, far_sq, far_mean, far_cols = opened(3, far_blocks, 2 * group_days)
+    mean_x = (joined_row(last, 0) + near_x + far_x) / total_days
+    var_x = (joined_row(last, 1) + near_sq + far_sq) / total_days - mean_x * mean_x
+    all_cols = own_cols + near_cols + far_cols
     mask = small[0:1, :]
     mask = mask + pltpu.roll(mask, 64, 1)
     inner = mask / (total_days * jnp.sqrt(var_x + 1e-06))
+    for k in range(half_k):
+        at = k * ROWS
+        far[at : at + ROWS, :] += (
+            joined(last, k)
+            + far_mean * pair_cols(far_cols, k)
+            - mean_x * pair_cols(all_cols, k)
+        )
 
     def normal(k):
-        value = joined(last, k) + far[k * ROWS : (k + 1) * ROWS, :]
-        value = value - mean_x * pair_cols(all_cols, k)
+        far_blocks[1 + k].wait_recv()
+        value = far[k * ROWS : (k + 1) * ROWS, :] + decoded(3, k)
         scale = jnp.where(low_row, outer[k : k + 1], outer[k + half_k : k + half_k + 1])
         return value * (inner * scale)
 
@@ -658,6 +663,7 @@
             pltpu.VMEM((groups, EXTRA + 16, 128), f32),
             pltpu.VMEM((half, 128), f32),
             pltpu.VMEM((half, 128), f32),
+            pltpu.VMEM((2, lanes, 128), jnp.bfloat16),
             pltpu.VMEM((kcount, 64, lag_list.shape[0]), f32),
             pltpu.VMEM((8, 128), f32),
             pltpu.VMEM((16, 128), f32),

time: 29.4 us -> 28.9 us (0.983); the launches traced: 28.9 us -> 28.8 us
  no operation moved by 1% of the time
where the time goes in v8:
time: 28.9 us; the launch traced here: 28.8 us
  Pallas kernels  27 us (93%)
  local copies, waits for them, and re-layouts  1.72 us (6%)
    pallas_call x1, Pallas kernels, shards(): pl.pallas_call(functools.partial(kernel, sizes), out_shape=jax.ShapeDtype...  27 us
    unnamed x1, local copies, waits for them, and re-layouts  1.72 us

profile of v8, /device:TPU:0, one launch (start us, length us, event | category | flops | bytes accessed | tf_op | source)
XLA Modules:
  0.0 28.8 jit_solution(15780842004512405112)
XLA Ops:
  0.0 27.0 %shard_map.55 = f32[10,64,61]{2,1,0:T(8,128)} custom-call(bf16[336,2048]{1,0:T(8,128)(2,1)} %field_hbm.1, f32[10,336]{1,0:T(8,128)} %bitcast.5, s32[1,61]{1,0:T(1,128)} %bitcast.6, s32[10]{0:T(128)} %offset_hbm.1, s32[1,64]{1,0:T(1,128)} %bitcast.7), custom_call_target="tpu_custom_call" | custom-call | tf_op jit(solution)/shard_map/pallas_call | solution.py:637
  27.0 1.7 %copy.7 = f32[64,10,61]{2,0,1:T(8,128)} copy(f32[64,10,61]{2,0,1:T(8,128)} %bitcast.4) | data formatting | bytes 312320

commit v9 on v8

--- a/solution.py
+++ b/solution.py
@@ -38,6 +38,8 @@
     mask_ref,
     field_ref,
     idx_ref,
+    pack_ref,
+    packs,
     idx_all,
     tiles,
     zmsg,
@@ -82,6 +84,11 @@
     lanes = idx_ref.shape[1]
     wide = lanes + 128
     half_k = kcount // 2
+    spare = [
+        ((row - 8) * (lanes // 128) + column, row, column * 128)
+        for row in range(8, kcount)
+        for column in range(lanes // 128)
+    ]
     count = half_k * ROWS
     cells = 128
     me = lax.axis_index("tm")
@@ -149,8 +156,8 @@
 
     def idx_copy(step):
         return remote(
-            idx_ref,
-            idx_all.at[m],
+            pack_ref,
+            packs.at[m],
             idx_send.at[0],
             idx_recv.at[step - 1],
             device_of(h, across(step)),
@@ -285,6 +292,10 @@
     tile = jnp.where(lane == 63, jnp.sum(series * series, 1, keepdims=True), tile)
     tiles[core * g + m] = tile
     idx_all[m] = series
+    pack_ref[:, :lanes] = series[:8]
+    pack_ref[:, lanes:] = jnp.zeros((8, 128), f32)
+    for at, row, column in spare:
+        pack_ref[at : at + 1, lanes:] = series[row : row + 1, column : column + 128]
 
     @pl.when(jnp.logical_not(has_edge))
     def _():
@@ -301,7 +312,7 @@
     small[0:1, 0 : cells // 2] = mask_ref[...].astype(f32)
     for piece in range(groups):
         own_copy(piece).start()
-        each(1, g, lambda s, piece=piece: raw_copy(piece, s).start())
+        each(1, g, lambda s, piece=piece: raw_copy(piece, g - s).start())
     for turn in range(groups - 2):
         tell_line(round_sem.at[turn])
         pl.semaphore_wait(round_sem.at[turn], beside)
@@ -315,7 +326,17 @@
     zero_tile = jnp.zeros((kcount, 128), f32)
     zmsg[...] = lax.fori_loop(0, 2 * g, lambda at, carry: carry + tiles[at], zero_tile)
     each(1, groups, lambda s: z_copy(s).start())
-    each(1, g, lambda s: idx_copy(s).wait_recv())
+
+    def unpack(step):
+        member = across(step)
+        idx_copy(step).wait_recv()
+        idx_all[member, 0:8, :] = packs[member, :, :lanes]
+        for at, row, column in spare:
+            idx_all[member, row : row + 1, column : column + 128] = packs[
+                member, at : at + 1, lanes:
+            ]
+
+    each(1, g, unpack)
 
     spot = lax.broadcasted_iota(jnp.int32, (kcount, wide), 1)
     wing = jnp.zeros((kcount, 128), f32)
@@ -364,39 +385,6 @@
     var = stats[:, 63:64] / total_days - mean * mean
     outer = 1.0 / jnp.sqrt(var + 1e-06)
 
-    place = lax.broadcasted_iota(jnp.int32, (kcount, lanes), 1)
-
-    def centered(value, valid):
-        return jnp.where(valid, (value - mean).astype(jnp.bfloat16).astype(f32), 0.0)
-
-    def center_body(at, carry):
-        return carry + centered(idx_all[at], place < t_dev)
-
-    core_sum = lax.fori_loop(0, g, center_body, jnp.zeros((kcount, lanes), f32))
-    inner_block = centered(idx_all[jnp.where(core == 0, 0, g - 1)], place < t_dev)
-    edge = jnp.concatenate([tiles[2 * g], tail[:, : lanes - 128]], 1)
-    edge = jnp.where(core == 0, pltpu.roll(edge, t_dev - 128, 1), edge)
-    opens = jnp.where(core == 0, t_dev - 64, 0)
-    closes = jnp.where(core == 0, t_dev, 62)
-    outer_block = centered(edge, (place >= opens) & (place < closes) & (edge < NEAR))
-
-    def part(value, side):
-        return jnp.dot(
-            value.astype(jnp.bfloat16), chooser[side], preferred_element_type=f32
-        )
-
-    by_shift = (
-        jnp.sum(core_sum, 1, keepdims=True)
-        + part(outer_block, 0)
-        - part(inner_block, 1)
-    )
-    tot_part[...] = jnp.zeros_like(tot_part)
-    for k in range(kcount):
-        tot_part[k : k + 1, :] = pltpu.roll(
-            by_shift[k : k + 1], lax.rem(128 - offset_ref[k], 128), 1
-        )
-    total_copy().start()
-
     def center_window(step):
         for k in range(kcount):
             value = raw_win[step, k * BASE : (k + 1) * BASE, :]
@@ -458,7 +446,8 @@
         own_copy(piece).wait()
         add([piece], 0, True)
 
-        def body(step, carry):
+        def body(turn, carry):
+            step = g - turn
             raw_copy(piece, step).wait_recv()
             add([piece], step, False)
             return carry
@@ -537,11 +526,50 @@
         add([0], step, first_time)
 
     early_body(0, True)
+
+    place = lax.broadcasted_iota(jnp.int32, (kcount, lanes), 1)
+
+    def centered(value, valid):
+        return jnp.where(valid, (value - mean).astype(jnp.bfloat16).astype(f32), 0.0)
+
+    def center_body(at, carry):
+        return carry + centered(idx_all[at], place < t_dev)
+
+    core_sum = jnp.zeros((kcount, lanes), f32)
+    if g <= 4:
+        for at in range(g):
+            core_sum = center_body(at, core_sum)
+    else:
+        core_sum = lax.fori_loop(0, g, center_body, core_sum)
+    inner_block = centered(idx_all[jnp.where(core == 0, 0, g - 1)], place < t_dev)
+    edge = jnp.concatenate([tiles[2 * g], tail[:, : lanes - 128]], 1)
+    edge = jnp.where(core == 0, pltpu.roll(edge, t_dev - 128, 1), edge)
+    opens = jnp.where(core == 0, t_dev - 64, 0)
+    closes = jnp.where(core == 0, t_dev, 62)
+    outer_block = centered(edge, (place >= opens) & (place < closes) & (edge < NEAR))
+
+    def part(value, side):
+        return jnp.dot(
+            value.astype(jnp.bfloat16), chooser[side], preferred_element_type=f32
+        )
+
+    by_shift = (
+        jnp.sum(core_sum, 1, keepdims=True)
+        + part(outer_block, 0)
+        - part(inner_block, 1)
+    )
+    tot_part[...] = jnp.zeros_like(tot_part)
+    for k in range(kcount):
+        tot_part[k : k + 1, :] = pltpu.roll(
+            by_shift[k : k + 1], lax.rem(128 - offset_ref[k], 128), 1
+        )
+
     if g <= 4:
         for step in range(1, g):
             early_body(step, False)
     else:
         each(1, g, lambda s: early_body(s, False))
+    total_copy().start()
     split(0, 0)
 
     total_copy().wait()
@@ -574,7 +602,7 @@
     all_cols = own_cols + near_cols + far_cols
     mask = small[0:1, :]
     mask = mask + pltpu.roll(mask, 64, 1)
-    inner = mask / (total_days * jnp.sqrt(var_x + 1e-06))
+    scaling = mask / (total_days * jnp.sqrt(var_x + 1e-06))
     for k in range(half_k):
         at = k * ROWS
         far[at : at + ROWS, :] += (
@@ -587,7 +615,7 @@
         far_blocks[1 + k].wait_recv()
         value = far[k * ROWS : (k + 1) * ROWS, :] + decoded(3, k)
         scale = jnp.where(low_row, outer[k : k + 1], outer[k + half_k : k + half_k + 1])
-        return value * (inner * scale)
+        return value * (scaling * scale)
 
     small_int = lag_ref[...] + MAXLAG
     small[0:1, 0 : lag_ref.shape[1]] = small_int.astype(f32)
@@ -610,7 +638,7 @@
     def drained(ref, sem):
         remote(ref, ref, sem, sem, partner).wait_send()
 
-    drained(idx_all.at[pl.ds(0, g - 1)], idx_send.at[0])
+    drained(packs.at[pl.ds(0, g - 1)], idx_send.at[0])
     drained(tiles.at[pl.ds(0, 2 * g - 1)], tile_send.at[0])
     drained(zin.at[pl.ds(0, groups - 1)], z_send.at[0])
     for piece in range(groups):
@@ -646,6 +674,8 @@
             pltpu.VMEM((1, sea_mask.shape[0]), jnp.int32),
             pltpu.VMEM((t_dev, cells_all), jnp.bfloat16),
             pltpu.VMEM((kcount, lanes), f32),
+            pltpu.VMEM((8, lanes + 128), f32),
+            pltpu.VMEM((g, 8, lanes + 128), f32),
             pltpu.VMEM((g, kcount, lanes), f32),
             pltpu.VMEM((2 * g + 1, kcount, 128), f32),
             pltpu.VMEM((kcount, 128), f32),

time: 28.9 us -> 29.3 us (1.014)
  the two profiles are of different devices: /device:TPU:0 before, /device:TPU:21 now
where the time goes in v9:
time: 29.3 us; the launch traced here: 29.2 us
  Pallas kernels  27.5 us (94%)
  local copies, waits for them, and re-layouts  1.72 us (6%)
    pallas_call x1, Pallas kernels, shards(): pl.pallas_call(functools.partial(kernel, sizes), out_shape=jax.ShapeDtype...  27.5 us
    unnamed x1, local copies, waits for them, and re-layouts  1.72 us

profile of v9, /device:TPU:21, one launch (start us, length us, event | category | flops | bytes accessed | tf_op | source)
XLA Modules:
  0.0 29.2 jit_solution(10022937379711893048)
XLA Ops:
  0.0 27.5 %shard_map.55 = f32[10,64,61]{2,1,0:T(8,128)} custom-call(bf16[336,2048]{1,0:T(8,128)(2,1)} %field_hbm.1, f32[10,336]{1,0:T(8,128)} %bitcast.5, s32[1,61]{1,0:T(1,128)} %bitcast.6, s32[10]{0:T(128)} %offset_hbm.1, s32[1,64]{1,0:T(1,128)} %bitcast.7), custom_call_target="tpu_custom_call" | custom-call | tf_op jit(solution)/shard_map/pallas_call | solution.py:665
  27.5 1.7 %copy.7 = f32[64,10,61]{2,0,1:T(8,128)} copy(f32[64,10,61]{2,0,1:T(8,128)} %bitcast.4) | data formatting | bytes 312320

commit v10 on v9

--- a/solution.py
+++ b/solution.py
@@ -312,7 +312,7 @@
     small[0:1, 0 : cells // 2] = mask_ref[...].astype(f32)
     for piece in range(groups):
         own_copy(piece).start()
-        each(1, g, lambda s, piece=piece: raw_copy(piece, g - s).start())
+        each(1, g, lambda s, piece=piece: raw_copy(piece, s).start())
     for turn in range(groups - 2):
         tell_line(round_sem.at[turn])
         pl.semaphore_wait(round_sem.at[turn], beside)
@@ -447,7 +447,7 @@
         add([piece], 0, True)
 
         def body(turn, carry):
-            step = g - turn
+            step = turn
             raw_copy(piece, step).wait_recv()
             add([piece], step, False)
             return carry

time: 29.3 us -> 28.6 us (0.976)
  the two profiles are of different devices: /device:TPU:21 before, /device:TPU:0 now
where the time goes in v10:
time: 28.6 us; the launch traced here: 28.4 us
  Pallas kernels  26.7 us (93%)
  local copies, waits for them, and re-layouts  1.72 us (6%)
    pallas_call x1, Pallas kernels, shards(): pl.pallas_call(functools.partial(kernel, sizes), out_shape=jax.ShapeDtype...  26.7 us
    unnamed x1, local copies, waits for them, and re-layouts  1.72 us

profile of v10, /device:TPU:0, one launch (start us, length us, event | category | flops | bytes accessed | tf_op | source)
XLA Modules:
  0.0 28.4 jit_solution(7101998678873722075)
XLA Ops:
  0.0 26.7 %shard_map.55 = f32[10,64,61]{2,1,0:T(8,128)} custom-call(bf16[336,2048]{1,0:T(8,128)(2,1)} %field_hbm.1, f32[10,336]{1,0:T(8,128)} %bitcast.5, s32[1,61]{1,0:T(1,128)} %bitcast.6, s32[10]{0:T(128)} %offset_hbm.1, s32[1,64]{1,0:T(1,128)} %bitcast.7), custom_call_target="tpu_custom_call" | custom-call | tf_op jit(solution)/shard_map/pallas_call | solution.py:665
  26.7 1.7 %copy.7 = f32[64,10,61]{2,0,1:T(8,128)} copy(f32[64,10,61]{2,0,1:T(8,128)} %bitcast.4) | data formatting | bytes 312320

commit v11 on v10

--- a/solution.py
+++ b/solution.py
@@ -191,13 +191,17 @@
             device_of(flipped(h, step, groups), m),
         )
 
-    def swap_copy(piece, k):
-        rows = pl.ds(k * ROWS, ROWS if k < half_k else EXTRA)
+    chunks = (half_k + 1) // 2
+
+    def swap_copy(piece, chunk):
+        begin = EXTRA + 2 * chunk * ROWS if chunk else 0
+        end = EXTRA + min(2 * chunk + 2, half_k) * ROWS
+        rows = pl.ds(begin, end - begin)
         return remote(
             other.at[piece, rows],
             partner_in.at[piece, rows],
             swap_send.at[piece],
-            swap_recv.at[piece, k],
+            swap_recv.at[piece, chunk],
             partner,
         )
 
@@ -215,18 +219,18 @@
                 sent_extra.at[piece],
                 got_extra.at[slot],
                 sum_send.at[1, piece],
-                sum_recv.at[half_k, slot],
+                sum_recv.at[chunks, slot],
                 receiver(piece),
             )
         ]
-        for k in range(half_k):
-            rows = pl.ds(k * ROWS, ROWS)
+        for chunk in range(chunks):
+            rows = pl.ds(2 * chunk * ROWS, min(2, half_k - 2 * chunk) * ROWS)
             copies.append(
                 remote(
                     sent.at[piece, rows],
                     got.at[slot, rows],
                     sum_send.at[0, piece],
-                    sum_recv.at[k, slot],
+                    sum_recv.at[chunk, slot],
                     receiver(piece),
                 )
             )
@@ -430,17 +434,17 @@
         for row in range(2):
             value = acc[sums_at + row : sums_at + row + 1, column]
             kept, given = halves(value, value, low_row)
-            mine[piece, count + row : count + row + 1, :] = kept
-            other[piece, count + row : count + row + 1, :] = given
-        swap_copy(piece, half_k).start()
+            mine[piece, row : row + 1, :] = kept
+            other[piece, row : row + 1, :] = given
         for k in range(half_k):
             at = k * ROWS
             kept, given = halves(
                 acc[at : at + ROWS, column], acc[count + at : count + at + ROWS, column], low
             )
-            mine[piece, at : at + ROWS, :] = kept
-            other[piece, at : at + ROWS, :] = given
-            swap_copy(piece, k).start()
+            mine[piece, EXTRA + at : EXTRA + at + ROWS, :] = kept
+            other[piece, EXTRA + at : EXTRA + at + ROWS, :] = given
+            if k % 2 == 1 or k == half_k - 1:
+                swap_copy(piece, k // 2).start()
 
     def products(piece):
         own_copy(piece).wait()
@@ -456,12 +460,13 @@
         split(piece, 0)
 
     def joined(piece, k):
-        at = k * ROWS
-        swap_copy(piece, k).wait_recv()
+        at = EXTRA + k * ROWS
+        if k % 2 == 0 and k > 0:
+            swap_copy(piece, k // 2).wait_recv()
         return mine[piece, at : at + ROWS, :] + partner_in[piece, at : at + ROWS, :]
 
     def joined_row(piece, row):
-        at = count + row
+        at = row
         return mine[piece, at : at + 1, :] + partner_in[piece, at : at + 1, :]
 
     def decoded(slot, k):
@@ -469,7 +474,7 @@
         return coded * (got_extra[slot, 2 + k : 3 + k, :] * (1.0 / TOP))
 
     def send_sums(piece, outer_slot):
-        swap_copy(piece, half_k).wait_recv()
+        swap_copy(piece, 0).wait_recv()
         sx, sq = joined_row(piece, 0), joined_row(piece, 1)
         tot, cols, days = own_tot, own_cols, group_days
         copies = sum_copies(piece, slot_of(piece))
@@ -499,13 +504,15 @@
         for k in range(half_k):
             value = stage[k * ROWS : (k + 1) * ROWS, :]
             if outer_slot is not None:
-                arriving[1 + k].wait_recv()
+                if k % 2 == 0:
+                    arriving[1 + k // 2].wait_recv()
                 value = value + decoded(outer_slot, k)
             scaled = value * (TOP / jnp.maximum(sent_extra[piece, 2 + k : 3 + k, :], 1e-30))
             sent[piece, k * ROWS : (k + 1) * ROWS, :] = (
                 jnp.round(scaled).astype(jnp.int32).astype(jnp.int16)
             )
-            copies[1 + k].start()
+            if k % 2 == 1 or k == half_k - 1:
+                copies[1 + k // 2].start()
 
     def send_outer(piece):
         @pl.when(jnp.logical_not(inner))
@@ -593,9 +600,10 @@
 
     near_x, near_sq, near_mean, near_cols = opened(2, near_blocks, group_days)
     for k in range(half_k):
-        near_blocks[1 + k].wait_recv()
+        if k % 2 == 0:
+            near_blocks[1 + k // 2].wait_recv()
         far[k * ROWS : (k + 1) * ROWS, :] = decoded(2, k) + near_mean * pair_cols(near_cols, k)
-    swap_copy(last, half_k).wait_recv()
+    swap_copy(last, 0).wait_recv()
     far_x, far_sq, far_mean, far_cols = opened(3, far_blocks, 2 * group_days)
     mean_x = (joined_row(last, 0) + near_x + far_x) / total_days
     var_x = (joined_row(last, 1) + near_sq + far_sq) / total_days - mean_x * mean_x
@@ -612,7 +620,8 @@
         )
 
     def normal(k):
-        far_blocks[1 + k].wait_recv()
+        if k % 2 == 0:
+            far_blocks[1 + k // 2].wait_recv()
         value = far[k * ROWS : (k + 1) * ROWS, :] + decoded(3, k)
         scale = jnp.where(low_row, outer[k : k + 1], outer[k + half_k : k + half_k + 1])
         return value * (scaling * scale)
@@ -708,9 +717,9 @@
             dma((1,)),
             dma((groups - 1,)),
             dma((groups,)),
-            dma((groups, kcount // 2 + 1)),
+            dma((groups, (kcount // 2 + 1) // 2)),
             dma((2, groups - 1)),
-            dma((kcount // 2 + 1, groups)),
+            dma(((kcount // 2 + 1) // 2 + 1, groups)),
             dma((groups + 1,)),
             pltpu.SemaphoreType.REGULAR((groups - 2,)),
             dma((1,)),

time: 28.6 us -> 28.1 us (0.983)
  Pallas kernels: 26.7 us -> 26 us
    pallas_call x1, Pallas kernels: 26.7 us -> 26 us  [shards(): pl.pallas_call(functools.partial(kernel, sizes), out_shape=jax.ShapeDtype...]
where the time goes in v11:
time: 28.1 us; the launch traced here: 27.7 us
  Pallas kernels  26 us (93%)
  local copies, waits for them, and re-layouts  1.72 us (6%)
    pallas_call x1, Pallas kernels, shards(): pl.pallas_call(functools.partial(kernel, sizes), out_shape=jax.ShapeDtype...  26 us
    unnamed x1, local copies, waits for them, and re-layouts  1.72 us

profile of v11, /device:TPU:0, one launch (start us, length us, event | category | flops | bytes accessed | tf_op | source)
XLA Modules:
  0.0 27.7 jit_solution(8616418392207627105)
XLA Ops:
  0.0 26.0 %shard_map.55 = f32[10,64,61]{2,1,0:T(8,128)} custom-call(bf16[336,2048]{1,0:T(8,128)(2,1)} %field_hbm.1, f32[10,336]{1,0:T(8,128)} %bitcast.5, s32[1,61]{1,0:T(1,128)} %bitcast.6, s32[10]{0:T(128)} %offset_hbm.1, s32[1,64]{1,0:T(1,128)} %bitcast.7), custom_call_target="tpu_custom_call" | custom-call | tf_op jit(solution)/shard_map/pallas_call | solution.py:674
  26.0 1.7 %copy.7 = f32[64,10,61]{2,0,1:T(8,128)} copy(f32[64,10,61]{2,0,1:T(8,128)} %bitcast.4) | data formatting | bytes 312320

commit v12 on v11

--- a/solution.py
+++ b/solution.py
@@ -306,6 +306,7 @@
         tiles[2 * g] = jnp.full((kcount, 128), FAR, f32)
 
     pl.semaphore_wait(barrier, 2 * g - 1 + beside + jnp.where(has_edge, 1, 0))
+    tell_line(round_sem.at[0])
 
     for side in range(2):
         each(1 - side, g, lambda s, side=side: tile_copy(side, s).start())
@@ -318,7 +319,8 @@
         own_copy(piece).start()
         each(1, g, lambda s, piece=piece: raw_copy(piece, s).start())
     for turn in range(groups - 2):
-        tell_line(round_sem.at[turn])
+        if turn > 0:
+            tell_line(round_sem.at[turn])
         pl.semaphore_wait(round_sem.at[turn], beside)
     for side in range(2):
         each(1 - side, g, lambda s, side=side: tile_copy(side, s).wait_recv())

time: 28.1 us -> 28.1 us (level)
  no operation moved by 1% of the time
where the time goes in v12:
time: 28.1 us; the launch traced here: 27.7 us
  Pallas kernels  26 us (93%)
  local copies, waits for them, and re-layouts  1.72 us (6%)
    pallas_call x1, Pallas kernels, shards(): pl.pallas_call(functools.partial(kernel, sizes), out_shape=jax.ShapeDtype...  26 us
    unnamed x1, local copies, waits for them, and re-layouts  1.72 us

profile of v12, /device:TPU:0, one launch (start us, length us, event | category | flops | bytes accessed | tf_op | source)
XLA Modules:
  0.0 27.7 jit_solution(8500224268653856829)
XLA Ops:
  0.0 26.0 %shard_map.55 = f32[10,64,61]{2,1,0:T(8,128)} custom-call(bf16[336,2048]{1,0:T(8,128)(2,1)} %field_hbm.1, f32[10,336]{1,0:T(8,128)} %bitcast.5, s32[1,61]{1,0:T(1,128)} %bitcast.6, s32[10]{0:T(128)} %offset_hbm.1, s32[1,64]{1,0:T(1,128)} %bitcast.7), custom_call_target="tpu_custom_call" | custom-call | tf_op jit(solution)/shard_map/pallas_call | solution.py:676
  26.0 1.7 %copy.7 = f32[64,10,61]{2,0,1:T(8,128)} copy(f32[64,10,61]{2,0,1:T(8,128)} %bitcast.4) | data formatting | bytes 312320
